TPU v7x, 32 devices: a whole 2x2x4 slice. The times are simulated.
32 devices in a mesh: blk: 8 (over z, core), section: 4 (over y, x).
Axes of the slice: x: 2, y: 2, z: 4, core: 2. Of those that a mesh axis runs over, the one named last changes fastest.
Arguments:
- hidden: bfloat16 [4, 2048, 4096], P('section', 'blk'), parts along dimension 1, may hold values from -6 to 6
- exit_layer: int32 [4096], P('blk'), parts along dimension 0, may hold values from 1 to 2
- lengths: int32 [4096], P('blk'), parts along dimension 0, may hold values from 1 to 16, as said below
- kv_cache: bfloat16 [4, 2048, 16, 256], P('section', 'blk'), parts along dimension 1, may hold values from -256 to 256
- norm_gain: bfloat16 [4, 4096], P('section'), may hold values from 0.5 to 1.5
- w_qkv: bfloat16 [4, 4096, 1280], P('section'), may hold values from -0.0625 to 0.0625
- w_out: bfloat16 [4, 1024, 4096], P('section'), may hold values from -0.1875 to 0.1875
Outputs:
- settled: bfloat16 [4096, 8192], P('blk', 'section'), parts along dimension 0
There are 8 independent parts, one for each index of `blk`. A program takes and returns all parts, laid end to end along the dimension named above; an argument that names none is the same for every part. Nothing has to cross between parts.
Inputs may be any that keep to these rules, and one draw needn't show every extreme that they name: `lengths`: some token has length 16.
All inputs are finite; a program needn't handle non-finite values.
Results may differ from a plain program's by a relative error of at most 0.03.
Values may be sent and summed in bfloat16 or wider, within the bound.
A program may use at most 64 MiB of HBM per device.

v0:
```python
import functools
import math

import jax
import jax.numpy as jnp
from jax import lax
from jax.experimental import pallas as pl
from jax.experimental.pallas import tpu as pltpu
from jax.sharding import PartitionSpec as P

BLOCK = 64
MICRO = 8


EPSILON = 1e-05
NEGATIVE = -1e30


def partner(value, axis, distance):
    return lax.ppermute(value, axis, [(i, i ^ 1 << distance) for i in range(lax.axis_size(axis))])


def shifted(value, axis, steps):
    count = lax.axis_size(axis)
    pairs = [(source, (source + steps) % count) for source in range(count)]
    return lax.ppermute(value, axis, pairs)


def body(hidden, exit_layer, lengths, kv_cache, norm_gain, w_qkv, w_out):
    devices = lax.axis_size("section")
    index = lax.axis_index("section")
    shards = max(2, devices // 4)
    cycle_size = devices // shards
    segment_bits = cycle_size.bit_length() - 1
    shard_bits = shards.bit_length() - 1
    segment_index = index // shards
    shard_index = index % shards
    own_blocks = hidden[0]
    gain_row = norm_gain[0].astype(jnp.float32)
    proj_weight = w_qkv[0]
    out_weight = w_out[0]
    cache_all = kv_cache[0]
    query_width = out_weight.shape[0]
    head_size = (proj_weight.shape[1] - query_width) // 2
    heads = query_width // head_size
    quarter = proj_weight.shape[0]
    total_width = quarter * shards
    group_rows = BLOCK // shards
    rounds = MICRO // cycle_size
    context = cache_all.shape[1]
    positions = jnp.arange(context, dtype=jnp.int32)
    blank_block = jnp.zeros((BLOCK, quarter), jnp.bfloat16)

    def advance(carry, microstep):
        incoming, arriving, records = carry
        micro_index = microstep - segment_index
        in_range = (micro_index >= 0) & (micro_index < MICRO)
        slot = jnp.clip(micro_index, 0, MICRO - 1)
        on_turn = microstep % cycle_size == 0
        local_slot = jnp.minimum(microstep // cycle_size, rounds - 1)
        own_block = lax.dynamic_slice_in_dim(own_blocks, local_slot * BLOCK, BLOCK, 0)
        exit_rows = lax.dynamic_slice_in_dim(exit_layer, slot * BLOCK, BLOCK)
        own_lengths = lax.dynamic_slice_in_dim(
            lengths, slot * BLOCK + shard_index * group_rows, group_rows
        )
        own_cache = lax.dynamic_slice_in_dim(cache_all, slot * group_rows, group_rows, 0)
        first_input = jnp.where(on_turn, own_block, arriving)
        entering = jnp.where(segment_index == 0, first_input, incoming)
        active = exit_rows > segment_index
        gate = in_range & (jnp.sum(active.astype(jnp.int32)) > 0)

        def local_partials():
            widened = entering.astype(jnp.float32)
            scaled = (widened * gain_row).astype(jnp.bfloat16)
            return (
                jnp.dot(scaled, proj_weight, preferred_element_type=jnp.float32),
                jnp.sum(widened * widened, axis=1),
            )

        def no_partials():
            return (
                jnp.zeros((BLOCK, proj_weight.shape[1]), jnp.float32),
                jnp.zeros((BLOCK,), jnp.float32),
            )

        partial_proj, partial_squares = lax.cond(gate, local_partials, no_partials)
        kept = (partial_proj, partial_squares)
        for level in range(shard_bits):
            bit = shard_bits - 1 - level
            upper = index >> bit & 1
            halves = tuple(
                (piece.reshape((2, piece.shape[0] // 2) + piece.shape[1:]) for piece in kept)
            )
            keep = tuple((jnp.where(upper == 1, half[1], half[0]) for half in halves))
            send = tuple((jnp.where(upper == 1, half[0], half[1]) for half in halves))
            received = partner(send, "section", bit)
            kept = tuple((first + second for first, second in zip(keep, received)))
        own_proj, own_squares = kept

        def local_attention():
            fitted = own_proj * lax.rsqrt(own_squares / total_width + EPSILON)[:, None]
            query = (fitted[:, :query_width] * (1.0 / math.sqrt(head_size))).astype(jnp.bfloat16)
            query = query.reshape(group_rows, heads, head_size)
            key_new = fitted[:, query_width : query_width + head_size].astype(jnp.bfloat16)
            value_new = fitted[:, query_width + head_size :].astype(jnp.bfloat16)
            scores = jnp.einsum(
                "rhd,rcd->rhc",
                query,
                own_cache[:, :, :head_size],
                preferred_element_type=jnp.float32,
            )
            own = jnp.einsum("rhd,rd->rh", query, key_new, preferred_element_type=jnp.float32)
            usable = (positions[None, :] < own_lengths[:, None])[:, None, :]
            scores = jnp.where(usable, scores, NEGATIVE)
            row_top = jnp.maximum(jnp.max(scores, axis=-1), own)
            raw = jnp.where(usable, jnp.exp(scores - row_top[:, :, None]), jnp.float32(0.0))
            raw_own = jnp.exp(own - row_top)
            total = jnp.sum(raw, axis=-1) + raw_own
            weights = (raw / total[:, :, None]).astype(jnp.bfloat16)
            own_weight = (raw_own / total).astype(jnp.bfloat16)
            attended = jnp.einsum(
                "rhc,rcd->rhd",
                weights,
                own_cache[:, :, head_size:],
                preferred_element_type=jnp.float32,
            )
            attended = (
                attended
                + own_weight.astype(jnp.float32)[:, :, None]
                * value_new.astype(jnp.float32)[:, None, :]
            )
            return attended.astype(jnp.bfloat16).reshape(group_rows, query_width)

        def no_attention():
            return jnp.zeros((group_rows, query_width), jnp.bfloat16)

        collected = lax.cond(gate, local_attention, no_attention)
        for level in range(shard_bits):
            bit = level
            other = partner(collected, "section", bit)
            upper = index >> bit & 1
            collected = jnp.where(
                upper == 1,
                jnp.concatenate([other, collected], 0),
                jnp.concatenate([collected, other], 0),
            )

        def local_update():
            branch_out = jnp.dot(collected, out_weight, preferred_element_type=jnp.float32)
            updated = (entering.astype(jnp.float32) + branch_out).astype(jnp.bfloat16)
            return jnp.where(active[:, None], updated, entering)

        def keep_state():
            return entering

        outgoing = lax.cond(gate, local_update, keep_state)
        leaving = in_range & (exit_rows == segment_index + 1)
        previous = lax.dynamic_slice_in_dim(records, slot * BLOCK, BLOCK, 0)
        records = lax.dynamic_update_slice_in_dim(
            records, jnp.where(leaving[:, None], outgoing, previous), slot * BLOCK, 0
        )
        relayed = jnp.where(on_turn & (segment_index > 0), own_block, arriving)
        incoming, arriving = shifted((outgoing, relayed), "section", shards)
        return ((incoming, arriving, records), None)

    start = (blank_block, blank_block, jnp.zeros((MICRO * BLOCK, quarter), jnp.bfloat16))
    carry, _ = lax.scan(advance, start, jnp.arange(MICRO + cycle_size - 1, dtype=jnp.int32))
    kept = carry[2]
    for level in range(segment_bits):
        bit = shard_bits + segment_bits - 1 - level
        upper = index >> bit & 1
        halves = kept.reshape(kept.shape[0], 2, kept.shape[1] // 2)
        keep = jnp.where(upper == 1, halves[:, 1], halves[:, 0])
        send = jnp.where(upper == 1, halves[:, 0], halves[:, 1])
        received = partner(send, "section", bit)
        kept = (keep.astype(jnp.float32) + received.astype(jnp.float32)).astype(jnp.bfloat16)
    return kept


MESH = pl.DeviceIdType.MESH


def cycle_kernel(
    sizes,
    hidden,
    tokens,
    cache_hbm,
    gain,
    wq_hbm,
    wo_hbm,
    out,
    wq,
    wo,
    cache,
    stage,
    ready,
    scaled,
    partial,
    squares,
    psend,
    precv,
    att,
    wx,
    att_in,
    load_sem,
    wy_send,
    wy_recv,
    wz_send,
    wz_recv,
    wd_send,
    wd_recv,
    own_sem,
    h_send,
    h_recv,
    lo_send,
    lo_recv,
    hi_send,
    hi_recv,
    p_send,
    p_recv,
    a_send,
    a_recv,
    r_send,
    r_recv,
    d_send,
    d_recv,
    keep_sem,
):
    shards, head_size, heads = sizes
    index = lax.axis_index("section")
    seg = index // shards
    shard = index % shards
    across = seg * shards + (1 - shard)
    along = (1 - seg) * shards + shard
    corner = (1 - seg) * shards + (1 - shard)
    width = stage.shape[2]
    columns = wq.shape[1]
    query_width = heads * head_size
    half = MICRO // 2
    rows = BLOCK // shards
    span = out.shape[1]
    context = cache.shape[1]
    own_rows = pl.ds(pl.multiple_of(shard * rows, rows), rows)
    other_rows = pl.ds(pl.multiple_of((1 - shard) * rows, rows), rows)

    place_blk = lax.axis_index("blk")
    chips = wz_send.shape[0] + 1
    chip = place_blk // 2
    core = place_blk % 2
    piece = wx.shape[0] // (2 * chips)

    def on_chip(steps):
        return (chip + steps + chips) % chips

    barrier = pltpu.get_barrier_semaphore()
    for peer in (across, along, corner):
        pl.semaphore_signal(barrier, inc=1, device_id={"section": peer}, device_id_type=MESH)
    for steps in range(1, chips):
        pl.semaphore_signal(
            barrier,
            inc=1,
            device_id={"blk": on_chip(steps) * 2 + core},
            device_id_type=MESH,
        )
    pl.semaphore_signal(
        barrier, inc=1, device_id={"blk": chip * 2 + 1 - core}, device_id_type=MESH
    )

    def piece_rows(owner):
        return pl.ds(pl.multiple_of(owner * piece, piece), piece)

    def weight_along():
        return pltpu.make_async_remote_copy(
            src_ref=wo_hbm.at[
                piece_rows(place_blk), pl.ds(pl.multiple_of((1 - seg) * span, 128), span)
            ],
            dst_ref=wx.at[piece_rows(place_blk)],
            send_sem=wy_send.at[0],
            recv_sem=wy_recv.at[0],
            device_id={"section": along},
            device_id_type=MESH,
        )

    def weight_chips(steps, owner):
        return pltpu.make_async_remote_copy(
            src_ref=wx.at[piece_rows(owner)],
            dst_ref=wx.at[piece_rows(owner)],
            send_sem=wz_send.at[steps - 1],
            recv_sem=wz_recv.at[steps - 1],
            device_id={"blk": on_chip(steps) * 2 + core},
            device_id_type=MESH,
        )

    def weight_cores(steps, owner):
        return pltpu.make_async_remote_copy(
            src_ref=wx.at[piece_rows(owner)],
            dst_ref=wx.at[piece_rows(owner)],
            send_sem=wd_send.at[steps],
            recv_sem=wd_recv.at[steps],
            device_id={"blk": chip * 2 + 1 - core},
            device_id_type=MESH,
        )

    def own_copy(i):
        return pltpu.make_async_copy(
            hidden.at[pl.ds(i * BLOCK, BLOCK)], stage.at[i], own_sem.at[i]
        )

    def rest_copy(i):
        return pltpu.make_async_copy(
            hidden.at[pl.ds(i * BLOCK, BLOCK), pl.ds(span, span)],
            stage.at[half + i, :, pl.ds(span, span)],
            own_sem.at[i],
        )

    load_wq = pltpu.make_async_copy(wq_hbm, wq, load_sem.at[0])
    load_cache = pltpu.make_async_copy(cache_hbm, cache, load_sem.at[1])
    load_wo = pltpu.make_async_copy(wo_hbm, wo, load_sem.at[2])

    @pl.when(seg == 0)
    def _():
        own_copy(0).start()

    load_wq.start()
    load_cache.start()

    def place(i):
        return jnp.where(i < half, 2 * i, 2 * (i - half) + 1)

    def hidden_copy(i):
        return pltpu.make_async_remote_copy(
            src_ref=hidden.at[pl.ds(i * BLOCK, BLOCK)],
            dst_ref=stage.at[half + i],
            send_sem=h_send.at[i],
            recv_sem=h_recv.at[i],
            device_id={"section": along},
            device_id_type=MESH,
        )

    def low_copy(i):
        return pltpu.make_async_remote_copy(
            src_ref=ready.at[i, :, pl.ds(0, span)],
            dst_ref=stage.at[i, :, pl.ds(0, span)],
            send_sem=lo_send.at[i],
            recv_sem=lo_recv.at[i],
            device_id={"section": along},
            device_id_type=MESH,
        )

    def high_copy(i):
        return pltpu.make_async_remote_copy(
            src_ref=ready.at[i, :, pl.ds(span, span)],
            dst_ref=stage.at[i, :, pl.ds(span, span)],
            send_sem=hi_send.at[i],
            recv_sem=hi_recv.at[i],
            device_id={"section": along},
            device_id_type=MESH,
        )

    def branch_copy(i, sent_rows):
        return pltpu.make_async_remote_copy(
            src_ref=att.at[i, sent_rows],
            dst_ref=att_in.at[i, sent_rows],
            send_sem=r_send.at[i],
            recv_sem=r_recv.at[i],
            device_id={"section": along},
            device_id_type=MESH,
        )

    def corner_copy(i, sent_rows):
        return pltpu.make_async_remote_copy(
            src_ref=att.at[i, sent_rows],
            dst_ref=att_in.at[i, sent_rows],
            send_sem=d_send.at[i],
            recv_sem=d_recv.at[i],
            device_id={"section": corner},
            device_id_type=MESH,
        )

    def partial_copy(i):
        return pltpu.make_async_remote_copy(
            src_ref=psend.at[i],
            dst_ref=precv.at[i],
            send_sem=p_send.at[i],
            recv_sem=p_recv.at[i],
            device_id={"section": across},
            device_id_type=MESH,
        )

    def attended_copy(i, sent_rows):
        return pltpu.make_async_remote_copy(
            src_ref=att.at[i, sent_rows],
            dst_ref=att.at[i, sent_rows],
            send_sem=a_send.at[i],
            recv_sem=a_recv.at[i],
            device_id={"section": across},
            device_id_type=MESH,
        )

    def out_rows(i):
        return pl.ds(pl.multiple_of(place(i) * BLOCK, BLOCK), BLOCK)

    def kept_copy(i):
        return pltpu.make_async_copy(
            ready.at[i, :, pl.ds(span, span)], out.at[out_rows(i)], keep_sem.at[i]
        )

    def final_copy(i):
        return pltpu.make_async_copy(
            stage.at[i, :, pl.ds(0, span)], out.at[out_rows(i)], keep_sem.at[i]
        )

    def spread():
        weight_along().wait_recv()
        for steps in range(1, chips):
            weight_chips(steps, place_blk).start()
        weight_cores(0, place_blk).start()

    def pass_on():
        for steps in range(1, chips):
            owner = on_chip(-steps) * 2 + core
            weight_chips(steps, owner).wait_recv()
            weight_cores(steps, owner).start()

    def gathered():
        for steps in range(chips):
            weight_cores(steps, on_chip(-steps) * 2 + 1 - core).wait_recv()

    pl.semaphore_wait(barrier, chips + 3)

    @pl.when(seg == 0)
    def _():
        weight_along().start()
        for i in range(1, half):
            own_copy(i).start()

    @pl.when(seg == 1)
    def _():
        hidden_copy(0).start()
        weight_along().start()
        for i in range(1, half):
            hidden_copy(i).start()
        for i in range(half):
            rest_copy(i).start()
        spread()

    def project(i):
        local = (seg == 0) & (i < half)

        @pl.when(local)
        def _():
            own_copy(i).wait()

        @pl.when((seg == 0) & (i == half))
        def _():
            spread()

        @pl.when((seg == 0) & (i >= half))
        def _():
            hidden_copy(i - half).wait_recv()

        @pl.when((seg == 1) & (i == half - 1))
        def _():
            pass_on()

        @pl.when((seg == 1) & (i < half))
        def _():
            high_copy(i).wait_recv()

        @pl.when((seg == 1) & (i == half))
        def _():
            gathered()

        @pl.when((seg == 1) & (i >= half))
        def _():
            rest_copy(i - half).wait()
            branch_copy(i, own_rows).wait_recv()
            corner_copy(i, other_rows).wait_recv()
            depth = tokens[pl.ds(pl.multiple_of(place(i) * BLOCK, BLOCK), BLOCK), :][:, 0:1]
            size = min(span, 512)
            for start in range(0, span, size):
                branch = jnp.dot(
                    att_in[i],
                    wx[:, pl.ds(start, size)],
                    preferred_element_type=jnp.float32,
                )
                cols = pl.ds(span + start, size)
                before = stage[i, :, cols].astype(jnp.float32)
                stage[i, :, cols] = jnp.where(depth > 0, before + branch, before).astype(
                    jnp.bfloat16
                )

        @pl.when(seg == 1)
        def _():
            low_copy(i).wait_recv()

        @pl.when(i == 0)
        def _():
            load_wq.wait()
            load_wo.start()

        chunk = min(width, 512)
        total = jnp.zeros((BLOCK, 1), jnp.float32)
        for start in range(0, width, chunk):
            cols = pl.ds(start, chunk)
            piece = stage[i, :, cols].astype(jnp.float32)
            total = total + jnp.sum(piece * piece, axis=1, keepdims=True)
            scaled[:, cols] = (piece * gain[:, cols].astype(jnp.float32)).astype(jnp.bfloat16)
        squares[...] = jnp.broadcast_to(total, squares.shape)
        step = 512
        for start in range(0, columns, step):
            cols = pl.ds(start, min(step, columns - start))
            partial[:, cols] = jnp.dot(
                scaled[...], wq[:, cols], preferred_element_type=jnp.float32
            )
        psend[i, :, pl.ds(0, columns)] = partial[other_rows, :].astype(jnp.bfloat16)
        theirs = squares[other_rows, :]
        coarse = theirs.astype(jnp.bfloat16)
        fine = (theirs - coarse.astype(jnp.float32)).astype(jnp.bfloat16)
        psend[i, :, pl.ds(columns, 128)] = coarse
        psend[i, :, pl.ds(columns + 128, 128)] = fine
        partial_copy(i).start()

    def attend_rows(i):
        @pl.when(i == 0)
        def _():
            load_cache.wait()

        partial_copy(i).wait_recv()
        coarse = precv[i, :, pl.ds(columns, 128)].astype(jnp.float32)
        fine = precv[i, :, pl.ds(columns + 128, 128)].astype(jnp.float32)
        total_squares = squares[own_rows, :] + coarse + fine
        factor = lax.rsqrt(total_squares / (width * shards) + EPSILON)[:, :1]
        fitted = (
            partial[own_rows, :] + precv[i, :, pl.ds(0, columns)].astype(jnp.float32)
        ) * factor
        scale = 1.0 / math.sqrt(head_size)
        query = jnp.concatenate(
            [fitted[:, h * head_size : (h + 1) * head_size] for h in range(heads)], axis=0
        )
        query = (query * scale).astype(jnp.bfloat16)
        key_new = fitted[:, query_width : query_width + head_size].astype(jnp.bfloat16)
        value_new = fitted[:, query_width + head_size :].astype(jnp.bfloat16)
        key_new = jnp.concatenate([key_new.astype(jnp.float32)] * heads, axis=0)
        value_new = jnp.concatenate([value_new.astype(jnp.float32)] * heads, axis=0)
        start = pl.multiple_of(place(i) * rows, rows)
        held = cache[pl.ds(start, rows)].reshape(rows * context, 2 * head_size)
        scores = lax.dot_general(
            query,
            held[:, :head_size],
            (((1,), (1,)), ((), ())),
            preferred_element_type=jnp.float32,
        )
        own = jnp.sum(query.astype(jnp.float32) * key_new, axis=1, keepdims=True)
        limits = tokens[pl.ds(pl.multiple_of(place(i) * BLOCK + shard * rows, rows), rows), :][:, 1:2]
        row = lax.broadcasted_iota(jnp.int32, (rows, 1), 0) * context
        low = jnp.concatenate([row] * heads, axis=0)
        high = jnp.concatenate([row + limits] * heads, axis=0)
        column = lax.broadcasted_iota(jnp.int32, scores.shape, 1)
        usable = (column >= low) & (column < high)
        scores = jnp.where(usable, scores, NEGATIVE)
        row_top = jnp.maximum(jnp.max(scores, axis=1, keepdims=True), own)
        raw = jnp.where(usable, jnp.exp(scores - row_top), 0.0)
        raw_own = jnp.exp(own - row_top)
        total = jnp.sum(raw, axis=1, keepdims=True) + raw_own
        weights = (raw / total).astype(jnp.bfloat16)
        own_weight = (raw_own / total).astype(jnp.bfloat16).astype(jnp.float32)
        attended = jnp.dot(
            weights, held[:, head_size:], preferred_element_type=jnp.float32
        )
        attended = (attended + own_weight * value_new).astype(jnp.bfloat16)
        att[i, own_rows, :] = jnp.concatenate(
            [attended[h * rows : (h + 1) * rows] for h in range(heads)], axis=1
        )
        attended_copy(i, own_rows).start()

        @pl.when((seg == 1) | (i >= half))
        def _():
            corner_copy(i, own_rows).start()
            branch_copy(i, own_rows).start()

    def update(i):
        @pl.when(i == 0)
        def _():
            load_wo.wait()

        attended_copy(i, other_rows).wait_recv()
        depth = tokens[pl.ds(pl.multiple_of(place(i) * BLOCK, BLOCK), BLOCK), :][:, 0:1]
        active = depth > seg
        step = min(span, 512)

        def fill(first):
            for start in range(first, first + span, step):
                cols = pl.ds(start, step)
                branch = jnp.dot(att[i], wo[:, cols], preferred_element_type=jnp.float32)
                before = stage[i, :, cols].astype(jnp.float32)
                ready[i, :, cols] = jnp.where(active, before + branch, before).astype(jnp.bfloat16)

        @pl.when(seg == 0)
        def _():
            fill(0)
            low_copy(i).start()

        @pl.when((seg == 1) | (i < half))
        def _():
            fill(span)

        @pl.when((seg == 0) & (i < half))
        def _():
            high_copy(i).start()

        @pl.when(seg == 1)
        def _():
            kept_copy(i).start()

    def step(i, carry):
        @pl.when(i < MICRO)
        def _():
            project(i)

        @pl.when(i > 0)
        def _():
            update(i - 1)

        @pl.when(i < MICRO)
        def _():
            attend_rows(i)

        return carry

    lax.fori_loop(0, MICRO + 1, step, 0)

    def finish(i, carry):
        branch_copy(i, own_rows).wait_recv()
        corner_copy(i, other_rows).wait_recv()
        depth = tokens[pl.ds(pl.multiple_of(place(i) * BLOCK, BLOCK), BLOCK), :][:, 0:1]
        size = min(span, 512)
        for start in range(0, span, size):
            cols = pl.ds(start, size)
            branch = jnp.dot(att_in[i], wx[:, cols], preferred_element_type=jnp.float32)
            before = ready[i, :, cols].astype(jnp.float32)
            stage[i, :, cols] = jnp.where(depth > 1, before + branch, before).astype(jnp.bfloat16)
        final_copy(i).start()
        return carry

    @pl.when(seg == 0)
    def _():
        pass_on()
        gathered()
        lax.fori_loop(0, MICRO, finish, 0)

    def drain(i, carry):
        partial_copy(i).wait_send()
        attended_copy(i, own_rows).wait_send()

        @pl.when(seg == 0)
        def _():
            low_copy(i).wait_send()
            final_copy(i).wait()

        @pl.when(seg == 1)
        def _():
            kept_copy(i).wait()

        @pl.when((seg == 1) | (i >= half))
        def _():
            branch_copy(i, own_rows).wait_send()
            corner_copy(i, own_rows).wait_send()

        return carry

    lax.fori_loop(0, MICRO, drain, 0)

    weight_along().wait_send()
    for steps in range(1, chips):
        weight_chips(steps, place_blk).wait_send()
    for steps in range(chips):
        weight_cores(steps, on_chip(-steps) * 2 + core).wait_send()

    @pl.when(seg == 0)
    def _():
        for i in range(half):
            high_copy(i).wait_send()

    @pl.when(seg == 1)
    def _():
        for i in range(half):
            hidden_copy(i).wait_send()


def cycle_of_two(chips, hidden, exit_layer, lengths, kv_cache, norm_gain, w_qkv, w_out):
    shards = 2
    width = w_qkv.shape[1]
    columns = w_qkv.shape[2]
    query_width = w_out.shape[1]
    head_size = (columns - query_width) // 2
    heads = query_width // head_size
    rows = BLOCK // shards
    tokens = jnp.stack([exit_layer, lengths], axis=1)
    any_space = pl.BlockSpec(memory_space=pl.ANY)
    vmem = pl.BlockSpec(memory_space=pltpu.VMEM)
    dma = pltpu.SemaphoreType.DMA((MICRO,))
    bf16 = jnp.bfloat16
    return pl.pallas_call(
        functools.partial(cycle_kernel, (shards, head_size, heads)),
        out_shape=jax.ShapeDtypeStruct((MICRO * BLOCK, width // 2), bf16),
        in_specs=[any_space, vmem, any_space, vmem, any_space, any_space],
        out_specs=any_space,
        scratch_shapes=[
            pltpu.VMEM(w_qkv.shape[1:], bf16),
            pltpu.VMEM(w_out.shape[1:], bf16),
            pltpu.VMEM(kv_cache.shape[1:], bf16),
            pltpu.VMEM((MICRO, BLOCK, width), bf16),
            pltpu.VMEM((MICRO, BLOCK, width), bf16),
            pltpu.VMEM((BLOCK, width), bf16),
            pltpu.VMEM((BLOCK, columns), jnp.float32),
            pltpu.VMEM((BLOCK, 128), jnp.float32),
            pltpu.VMEM((MICRO, rows, columns + 256), bf16),
            pltpu.VMEM((MICRO, rows, columns + 256), bf16),
            pltpu.VMEM((MICRO, BLOCK, query_width), bf16),
            pltpu.VMEM((query_width, width // 2), bf16),
            pltpu.VMEM((MICRO, BLOCK, query_width), bf16),
            pltpu.SemaphoreType.DMA((3,)),
            pltpu.SemaphoreType.DMA((1,)),
            pltpu.SemaphoreType.DMA((1,)),
            pltpu.SemaphoreType.DMA((chips - 1,)),
            pltpu.SemaphoreType.DMA((chips - 1,)),
            pltpu.SemaphoreType.DMA((chips,)),
            pltpu.SemaphoreType.DMA((chips,)),
        ]
        + [dma] * 16,
        compiler_params=pltpu.CompilerParams(
            collective_id=0, has_side_effects=True, vmem_limit_bytes=60 << 20
        ),
        name="cycle",
    )(hidden[0], tokens, kv_cache[0], norm_gain, w_qkv[0], w_out[0])


def chosen(batches, devices, *arguments):
    shards = max(2, devices // 4)
    if shards == 2 and devices // shards == 2:
        return cycle_of_two(batches // 2, *arguments)
    return body(*arguments)


def solution(mesh):
    return jax.shard_map(
        functools.partial(chosen, mesh.shape["blk"], mesh.shape["section"]),
        mesh=mesh,
        in_specs=(
            P("section", "blk", None),
            P("blk"),
            P("blk"),
            P("section", "blk", None, None),
            P("section", None),
            P("section", None, None),
            P("section", None, None),
        ),
        out_specs=P("blk", "section"),
        check_vma=False,
    )
```

profile of v0, /device:TPU:0, one launch (start us, length us, event | category | flops | bytes accessed | tf_op | source)
XLA Modules:
  0.0 119.4 jit_solution(4287008868200046789)
XLA Ops:
  0.0 0.7 pad_add_fusion
  0.7 0.9 copy.10.tokens
  1.6 114.6 %cycle.1 = bf16[512,2048]{1,0:T(8,128)(2,1)} custom-call(bf16[256,4096]{1,0:T(8,128)(2,1)} %bitcast.8, s32[512,2]{1,0:T(8,128)} %copy.10.tokens, bf16[256,16,256]{2,1,0:T(8,128)(2,1)} %bitcast.9, bf16[1,4096]{1,0:T(2,128)(2,1)} %gain.1, bf16[4096,1280]{1,0:T(8,128)(2,1)} %bitcast.6, bf16[1024,4096]{1,0:T(8,128)(2,1)} %bitcast.7), custom_call_target="tpu_custom_call" | custom-call | tf_op jit(solution)/shard_map/cycle/pallas_call | solution.py:704
  116.2 3.2 %copy.12 = bf16[512,2048]{1,0:T(8,128)(2,1)} copy(bf16[512,2048]{1,0:T(8,128)(2,1)} %cycle.1) | data formatting | bytes 4194304
where the time goes:
time: 120 us; the launch traced here: 119 us
  Pallas kernels  115 us (96%)
  local copies, waits for them, and re-layouts  4.02 us (3%)
    pallas_call x1, Pallas kernels, cycle_of_two(): pl.pallas_call(functools.partial(cycle_kernel, (shards, head_size, heads)...  115 us
    unnamed x1, local copies, waits for them, and re-layouts  3.16 us

commit v1 on v0

v1 whole, which is shorter than its diff:
```python
import functools
import math

import jax
import jax.numpy as jnp
from jax import lax
from jax.experimental import pallas as pl
from jax.experimental.pallas import tpu as pltpu
from jax.sharding import PartitionSpec as P

BLOCK = 64
MICRO = 8


EPSILON = 1e-05
NEGATIVE = -1e30
VMEM_LIMIT = 60 << 20


def partner(value, axis, distance):
    return lax.ppermute(value, axis, [(i, i ^ 1 << distance) for i in range(lax.axis_size(axis))])


def shifted(value, axis, steps):
    count = lax.axis_size(axis)
    pairs = [(source, (source + steps) % count) for source in range(count)]
    return lax.ppermute(value, axis, pairs)


def body(hidden, exit_layer, lengths, kv_cache, norm_gain, w_qkv, w_out):
    devices = lax.axis_size("section")
    index = lax.axis_index("section")
    shards = max(2, devices // 4)
    cycle_size = devices // shards
    segment_bits = cycle_size.bit_length() - 1
    shard_bits = shards.bit_length() - 1
    segment_index = index // shards
    shard_index = index % shards
    own_blocks = hidden[0]
    gain_row = norm_gain[0].astype(jnp.float32)
    proj_weight = w_qkv[0]
    out_weight = w_out[0]
    cache_all = kv_cache[0]
    query_width = out_weight.shape[0]
    head_size = (proj_weight.shape[1] - query_width) // 2
    heads = query_width // head_size
    quarter = proj_weight.shape[0]
    total_width = quarter * shards
    group_rows = BLOCK // shards
    rounds = MICRO // cycle_size
    context = cache_all.shape[1]
    positions = jnp.arange(context, dtype=jnp.int32)
    blank_block = jnp.zeros((BLOCK, quarter), jnp.bfloat16)

    def advance(carry, microstep):
        incoming, arriving, records = carry
        micro_index = microstep - segment_index
        in_range = (micro_index >= 0) & (micro_index < MICRO)
        slot = jnp.clip(micro_index, 0, MICRO - 1)
        on_turn = microstep % cycle_size == 0
        local_slot = jnp.minimum(microstep // cycle_size, rounds - 1)
        own_block = lax.dynamic_slice_in_dim(own_blocks, local_slot * BLOCK, BLOCK, 0)
        exit_rows = lax.dynamic_slice_in_dim(exit_layer, slot * BLOCK, BLOCK)
        own_lengths = lax.dynamic_slice_in_dim(
            lengths, slot * BLOCK + shard_index * group_rows, group_rows
        )
        own_cache = lax.dynamic_slice_in_dim(cache_all, slot * group_rows, group_rows, 0)
        first_input = jnp.where(on_turn, own_block, arriving)
        entering = jnp.where(segment_index == 0, first_input, incoming)
        active = exit_rows > segment_index
        gate = in_range & (jnp.sum(active.astype(jnp.int32)) > 0)

        def local_partials():
            widened = entering.astype(jnp.float32)
            scaled = (widened * gain_row).astype(jnp.bfloat16)
            return (
                jnp.dot(scaled, proj_weight, preferred_element_type=jnp.float32),
                jnp.sum(widened * widened, axis=1),
            )

        def no_partials():
            return (
                jnp.zeros((BLOCK, proj_weight.shape[1]), jnp.float32),
                jnp.zeros((BLOCK,), jnp.float32),
            )

        partial_proj, partial_squares = lax.cond(gate, local_partials, no_partials)
        kept = (partial_proj, partial_squares)
        for level in range(shard_bits):
            bit = shard_bits - 1 - level
            upper = index >> bit & 1
            halves = tuple(
                (piece.reshape((2, piece.shape[0] // 2) + piece.shape[1:]) for piece in kept)
            )
            keep = tuple((jnp.where(upper == 1, half[1], half[0]) for half in halves))
            send = tuple((jnp.where(upper == 1, half[0], half[1]) for half in halves))
            received = partner(send, "section", bit)
            kept = tuple((first + second for first, second in zip(keep, received)))
        own_proj, own_squares = kept

        def local_attention():
            fitted = own_proj * lax.rsqrt(own_squares / total_width + EPSILON)[:, None]
            query = (fitted[:, :query_width] * (1.0 / math.sqrt(head_size))).astype(jnp.bfloat16)
            query = query.reshape(group_rows, heads, head_size)
            key_new = fitted[:, query_width : query_width + head_size].astype(jnp.bfloat16)
            value_new = fitted[:, query_width + head_size :].astype(jnp.bfloat16)
            scores = jnp.einsum(
                "rhd,rcd->rhc",
                query,
                own_cache[:, :, :head_size],
                preferred_element_type=jnp.float32,
            )
            own = jnp.einsum("rhd,rd->rh", query, key_new, preferred_element_type=jnp.float32)
            usable = (positions[None, :] < own_lengths[:, None])[:, None, :]
            scores = jnp.where(usable, scores, NEGATIVE)
            row_top = jnp.maximum(jnp.max(scores, axis=-1), own)
            raw = jnp.where(usable, jnp.exp(scores - row_top[:, :, None]), jnp.float32(0.0))
            raw_own = jnp.exp(own - row_top)
            total = jnp.sum(raw, axis=-1) + raw_own
            weights = (raw / total[:, :, None]).astype(jnp.bfloat16)
            own_weight = (raw_own / total).astype(jnp.bfloat16)
            attended = jnp.einsum(
                "rhc,rcd->rhd",
                weights,
                own_cache[:, :, head_size:],
                preferred_element_type=jnp.float32,
            )
            attended = (
                attended
                + own_weight.astype(jnp.float32)[:, :, None]
                * value_new.astype(jnp.float32)[:, None, :]
            )
            return attended.astype(jnp.bfloat16).reshape(group_rows, query_width)

        def no_attention():
            return jnp.zeros((group_rows, query_width), jnp.bfloat16)

        collected = lax.cond(gate, local_attention, no_attention)
        for level in range(shard_bits):
            bit = level
            other = partner(collected, "section", bit)
            upper = index >> bit & 1
            collected = jnp.where(
                upper == 1,
                jnp.concatenate([other, collected], 0),
                jnp.concatenate([collected, other], 0),
            )

        def local_update():
            branch_out = jnp.dot(collected, out_weight, preferred_element_type=jnp.float32)
            updated = (entering.astype(jnp.float32) + branch_out).astype(jnp.bfloat16)
            return jnp.where(active[:, None], updated, entering)

        def keep_state():
            return entering

        outgoing = lax.cond(gate, local_update, keep_state)
        leaving = in_range & (exit_rows == segment_index + 1)
        previous = lax.dynamic_slice_in_dim(records, slot * BLOCK, BLOCK, 0)
        records = lax.dynamic_update_slice_in_dim(
            records, jnp.where(leaving[:, None], outgoing, previous), slot * BLOCK, 0
        )
        relayed = jnp.where(on_turn & (segment_index > 0), own_block, arriving)
        incoming, arriving = shifted((outgoing, relayed), "section", shards)
        return ((incoming, arriving, records), None)

    start = (blank_block, blank_block, jnp.zeros((MICRO * BLOCK, quarter), jnp.bfloat16))
    carry, _ = lax.scan(advance, start, jnp.arange(MICRO + cycle_size - 1, dtype=jnp.int32))
    kept = carry[2]
    for level in range(segment_bits):
        bit = shard_bits + segment_bits - 1 - level
        upper = index >> bit & 1
        halves = kept.reshape(kept.shape[0], 2, kept.shape[1] // 2)
        keep = jnp.where(upper == 1, halves[:, 1], halves[:, 0])
        send = jnp.where(upper == 1, halves[:, 0], halves[:, 1])
        received = partner(send, "section", bit)
        kept = (keep.astype(jnp.float32) + received.astype(jnp.float32)).astype(jnp.bfloat16)
    return kept


MESH = pl.DeviceIdType.MESH
CHUNKS = 2


def cycle_kernel(
    sizes,
    hidden,
    exits,
    lens,
    cache_hbm,
    gain,
    wq_hbm,
    wo_hbm,
    out,
    wq,
    wo,
    cache,
    stage,
    ready,
    table,
    scaled,
    partial,
    squares,
    psend,
    precv,
    att,
    wx,
    att_in,
    load_sem,
    own_sem,
    wy_send,
    wy_recv,
    up_send,
    up_recv,
    dn_send,
    dn_recv,
    wd_send,
    wd_recv,
    h_send,
    h_recv,
    lo_send,
    lo_recv,
    hi_send,
    hi_recv,
    p_send,
    p_recv,
    a_send,
    a_recv,
    r_send,
    r_recv,
    d_send,
    d_recv,
    x_send,
    x_recv,
):
    shards, head_size, heads = sizes
    index = lax.axis_index("section")
    seg = index // shards
    shard = index % shards
    across = seg * shards + (1 - shard)
    along = (1 - seg) * shards + shard
    corner = (1 - seg) * shards + (1 - shard)
    width = stage.shape[2]
    columns = wq.shape[1]
    query_width = heads * head_size
    half = MICRO // 2
    rows = BLOCK // shards
    span = out.shape[1]
    wide = wx.shape[1]
    low = width - wide
    context = cache.shape[1]
    own_rows = pl.ds(pl.multiple_of(shard * rows, rows), rows)
    other_rows = pl.ds(pl.multiple_of((1 - shard) * rows, rows), rows)

    place_blk = lax.axis_index("blk")
    chips = wd_send.shape[0]
    chip = place_blk // 2
    core = place_blk % 2
    chunk_rows = wx.shape[0] // (2 * chips * CHUNKS)
    above = jnp.minimum(chip + 1, chips - 1) * 2 + core
    below = jnp.maximum(chip - 1, 0) * 2 + core
    beside = chip * 2 + 1 - core
    has_above = chip < chips - 1
    has_below = chip > 0

    def remote(source, target, send, recv, device):
        return pltpu.make_async_remote_copy(
            src_ref=source,
            dst_ref=target,
            send_sem=send,
            recv_sem=recv,
            device_id=device,
            device_id_type=MESH,
        )

    barrier = pltpu.get_barrier_semaphore()
    for peer in (across, along, corner):
        pl.semaphore_signal(barrier, inc=1, device_id={"section": peer}, device_id_type=MESH)

    @pl.when(has_above)
    def _():
        pl.semaphore_signal(barrier, inc=1, device_id={"blk": above}, device_id_type=MESH)

    @pl.when(has_below)
    def _():
        pl.semaphore_signal(barrier, inc=1, device_id={"blk": below}, device_id_type=MESH)

    pl.semaphore_signal(barrier, inc=1, device_id={"blk": beside}, device_id_type=MESH)

    def own_copy(i):
        return pltpu.make_async_copy(
            hidden.at[pl.ds(i * BLOCK, BLOCK)], stage.at[i], own_sem.at[i]
        )

    def rest_copy(i):
        return pltpu.make_async_copy(
            hidden.at[pl.ds(i * BLOCK, BLOCK), pl.ds(low, wide)],
            stage.at[half + i, :, pl.ds(low, wide)],
            own_sem.at[i],
        )

    load_wq = pltpu.make_async_copy(wq_hbm, wq, load_sem.at[0])
    load_cache = pltpu.make_async_copy(cache_hbm, cache, load_sem.at[1])
    load_wo = pltpu.make_async_copy(wo_hbm, wo, load_sem.at[2])

    @pl.when(seg == 0)
    def _():
        own_copy(0).start()

    load_wq.start()
    load_cache.start()

    lane = lax.broadcasted_iota(jnp.int32, (128, 128), 1)
    line = lax.broadcasted_iota(jnp.int32, (128, 128), 0)
    for start in range(0, MICRO * BLOCK, 128):
        cols = pl.ds(start, 128)
        depth = jnp.sum(jnp.where(lane == line, exits[:, cols], 0), axis=1, keepdims=True)
        limit = jnp.sum(jnp.where(lane == line, lens[:, cols], 0), axis=1, keepdims=True)
        table[cols, :] = jnp.where(lane == 0, depth, limit)

    def place(i):
        return jnp.where(i < half, 2 * i, 2 * (i - half) + 1)

    def token_rows(i):
        return pl.ds(pl.multiple_of(place(i) * BLOCK, BLOCK), BLOCK)

    def depths(i):
        return table[token_rows(i), :][:, 0:1]

    def chunk_at(owner, chunk):
        first = pl.multiple_of(owner * (CHUNKS * chunk_rows) + chunk * chunk_rows, chunk_rows)
        return pl.ds(first, chunk_rows)

    def weight_out(layer, chunk):
        at = chunk_at(place_blk, chunk)
        first, size = (low, wide) if layer == 0 else (0, span)
        return remote(
            wo_hbm.at[at, pl.ds(first, size)],
            wx.at[at, pl.ds(0, size)],
            wy_send.at[chunk],
            wy_recv.at[chunk],
            {"section": along},
        )

    def held_size(layer):
        return pl.ds(0, wide if layer == 1 else span)

    def weight_in(layer, chunk):
        part = wx.at[chunk_at(place_blk, chunk), held_size(layer)]
        return remote(part, part, wy_send.at[chunk], wy_recv.at[chunk], {"section": along})

    def upward(layer, owner, chunk):
        part = wx.at[chunk_at(owner * 2 + core, chunk), held_size(layer)]
        return remote(
            part, part, up_send.at[owner, chunk], up_recv.at[owner, chunk], {"blk": above}
        )

    def downward(layer, owner, chunk):
        part = wx.at[chunk_at(owner * 2 + core, chunk), held_size(layer)]
        return remote(
            part, part, dn_send.at[owner, chunk], dn_recv.at[owner, chunk], {"blk": below}
        )

    def sideways(layer, owner, chunk, holder):
        part = wx.at[chunk_at(owner * 2 + holder, chunk), held_size(layer)]
        return remote(
            part, part, wd_send.at[owner, chunk], wd_recv.at[owner, chunk], {"blk": beside}
        )

    def spread(layer, chunk):
        weight_in(layer, chunk).wait_recv()

        @pl.when(has_above)
        def _():
            upward(layer, chip, chunk).start()

        @pl.when(has_below)
        def _():
            downward(layer, chip, chunk).start()

        sideways(layer, chip, chunk, core).start()

    def pass_on(layer, distance, chunk):
        @pl.when(chip >= distance)
        def _():
            upward(layer, chip - distance, chunk).wait_recv()

            @pl.when(has_above)
            def _():
                upward(layer, chip - distance, chunk).start()

            sideways(layer, chip - distance, chunk, core).start()

        @pl.when(chip + distance < chips)
        def _():
            downward(layer, chip + distance, chunk).wait_recv()

            @pl.when(has_below)
            def _():
                downward(layer, chip + distance, chunk).start()

            sideways(layer, chip + distance, chunk, core).start()

    def gathered(layer):
        for owner in range(chips):
            for chunk in range(CHUNKS):
                sideways(layer, owner, chunk, 1 - core).wait_recv()

    def settle_weights(layer):
        for chunk in range(CHUNKS):
            weight_out(layer, chunk).wait_send()
            for owner in range(chips):
                sideways(layer, owner, chunk, core).wait_send()

                @pl.when(has_above & (owner <= chip))
                def _():
                    upward(layer, owner, chunk).wait_send()

                @pl.when(has_below & (owner >= chip))
                def _():
                    downward(layer, owner, chunk).wait_send()

    def hidden_copy(i):
        return remote(
            hidden.at[pl.ds(i * BLOCK, BLOCK)],
            stage.at[half + i],
            h_send.at[i],
            h_recv.at[i],
            {"section": along},
        )

    def low_copy(i, size):
        return remote(
            ready.at[i, :, pl.ds(0, size)],
            stage.at[i, :, pl.ds(0, size)],
            lo_send.at[i],
            lo_recv.at[i],
            {"section": along},
        )

    def high_copy(i):
        cols = pl.ds(span, span)
        return remote(
            ready.at[i, :, cols],
            stage.at[i, :, cols],
            hi_send.at[i],
            hi_recv.at[i],
            {"section": along},
        )

    def branch_copy(i, sent_rows):
        return remote(
            att.at[i, sent_rows],
            att_in.at[i, sent_rows],
            r_send.at[i],
            r_recv.at[i],
            {"section": along},
        )

    def corner_copy(i, sent_rows):
        return remote(
            att.at[i, sent_rows],
            att_in.at[i, sent_rows],
            d_send.at[i],
            d_recv.at[i],
            {"section": corner},
        )

    def relay_copy(i, sent_rows):
        return remote(
            att_in.at[i, sent_rows],
            att_in.at[i, sent_rows],
            x_send.at[i],
            x_recv.at[i],
            {"section": across},
        )

    def partial_copy(i):
        return remote(
            psend.at[i], precv.at[i], p_send.at[i], p_recv.at[i], {"section": across}
        )

    def attended_copy(i, sent_rows):
        return remote(
            att.at[i, sent_rows],
            att.at[i, sent_rows],
            a_send.at[i],
            a_recv.at[i],
            {"section": across},
        )

    def scale(i, first, last):
        total = jnp.zeros((BLOCK, 1), jnp.float32)
        size = min(last - first, 512)
        for start in range(first, last, size):
            cols = pl.ds(start, size)
            piece = stage[i, :, cols].astype(jnp.float32)
            total = total + jnp.sum(piece * piece, axis=1, keepdims=True)
            scaled[:, cols] = (piece * gain[:, cols].astype(jnp.float32)).astype(jnp.bfloat16)
        return total

    def multiply(first, last, more):
        step = 512
        for start in range(0, columns, step):
            cols = pl.ds(start, min(step, columns - start))
            product = jnp.dot(
                scaled[:, pl.ds(first, last - first)],
                wq[pl.ds(first, last - first), cols],
                preferred_element_type=jnp.float32,
            )
            partial[:, cols] = partial[:, cols] + product if more else product

    def send_partial(i):
        psend[i, :, pl.ds(0, columns)] = partial[other_rows, :].astype(jnp.bfloat16)
        theirs = squares[other_rows, :]
        coarse = theirs.astype(jnp.bfloat16)
        fine = (theirs - coarse.astype(jnp.float32)).astype(jnp.bfloat16)
        psend[i, :, pl.ds(columns, 128)] = coarse
        psend[i, :, pl.ds(columns + 128, 128)] = fine
        partial_copy(i).start()

    def project(i):
        squares[...] = jnp.broadcast_to(scale(i, 0, width), squares.shape)
        multiply(0, width, False)
        send_partial(i)

    def attend_rows(i):
        partial_copy(i).wait_recv()
        coarse = precv[i, :, pl.ds(columns, 128)].astype(jnp.float32)
        fine = precv[i, :, pl.ds(columns + 128, 128)].astype(jnp.float32)
        total_squares = squares[own_rows, :] + coarse + fine
        factor = lax.rsqrt(total_squares / (width * shards) + EPSILON)[:, :1]
        fitted = (
            partial[own_rows, :] + precv[i, :, pl.ds(0, columns)].astype(jnp.float32)
        ) * factor
        scale = 1.0 / math.sqrt(head_size)
        query = jnp.concatenate(
            [fitted[:, h * head_size : (h + 1) * head_size] for h in range(heads)], axis=0
        )
        query = (query * scale).astype(jnp.bfloat16)
        key_new = fitted[:, query_width : query_width + head_size].astype(jnp.bfloat16)
        value_new = fitted[:, query_width + head_size :].astype(jnp.bfloat16)
        key_new = jnp.concatenate([key_new.astype(jnp.float32)] * heads, axis=0)
        value_new = jnp.concatenate([value_new.astype(jnp.float32)] * heads, axis=0)
        start = pl.multiple_of(place(i) * rows, rows)
        held = cache[pl.ds(start, rows)].reshape(rows * context, 2 * head_size)
        scores = lax.dot_general(
            query,
            held[:, :head_size],
            (((1,), (1,)), ((), ())),
            preferred_element_type=jnp.float32,
        )
        own = jnp.sum(query.astype(jnp.float32) * key_new, axis=1, keepdims=True)
        limits = table[pl.ds(pl.multiple_of(place(i) * BLOCK + shard * rows, rows), rows), :][:, 1:2]
        row = lax.broadcasted_iota(jnp.int32, (rows, 1), 0) * context
        first = jnp.concatenate([row] * heads, axis=0)
        last = jnp.concatenate([row + limits] * heads, axis=0)
        column = lax.broadcasted_iota(jnp.int32, scores.shape, 1)
        usable = (column >= first) & (column < last)
        scores = jnp.where(usable, scores, NEGATIVE)
        row_top = jnp.maximum(jnp.max(scores, axis=1, keepdims=True), own)
        raw = jnp.where(usable, jnp.exp(scores - row_top), 0.0)
        raw_own = jnp.exp(own - row_top)
        total = jnp.sum(raw, axis=1, keepdims=True) + raw_own
        weights = (raw / total).astype(jnp.bfloat16)
        own_weight = (raw_own / total).astype(jnp.bfloat16).astype(jnp.float32)
        attended = jnp.dot(
            weights, held[:, head_size:], preferred_element_type=jnp.float32
        )
        attended = (attended + own_weight * value_new).astype(jnp.bfloat16)
        att[i, own_rows, :] = jnp.concatenate(
            [attended[h * rows : (h + 1) * rows] for h in range(heads)], axis=1
        )

    def added(source, weight, before, chosen, target, first, last, shift_weight, shift):
        size = min(last - first, 512)
        for start in range(first, last, size):
            branch = jnp.dot(
                source,
                weight[:, pl.ds(start + shift_weight, size)],
                preferred_element_type=jnp.float32,
            )
            kept = before[:, pl.ds(start, size)].astype(jnp.float32)
            target[:, pl.ds(start + shift, size)] = jnp.where(
                chosen, kept + branch, kept
            ).astype(jnp.bfloat16)

    pl.semaphore_wait(
        barrier, 4 + has_above.astype(jnp.int32) + has_below.astype(jnp.int32)
    )

    def first_layer():
        for chunk in range(CHUNKS):
            weight_out(0, chunk).start()
        for i in range(1, half):
            own_copy(i).start()
        load_wo.start()

        def update(i):
            attended_copy(i, other_rows).wait_recv()
            active = depths(i) > 0
            fill = functools.partial(added, att[i], wo, stage.at[i], active, ready.at[i])
            fill(0, span, 0, 0)

            @pl.when(i < half)
            def _():
                low_copy(i, span).start()
                fill(span, width, 0, 0)
                high_copy(i).start()

            if low:

                @pl.when(i >= half)
                def _():
                    low_copy(i, low).start()

        def step(i, carry):
            @pl.when(i < MICRO)
            def _():
                @pl.when(i < half)
                def _():
                    own_copy(i).wait()

                @pl.when(i == half)
                def _():
                    for chunk in range(CHUNKS):
                        spread(0, chunk)

                @pl.when(i >= half)
                def _():
                    hidden_copy(i - half).wait_recv()

                for distance in range(1, chips - 1):

                    @pl.when(i == half + 1 + distance)
                    def _():
                        for chunk in range(CHUNKS):
                            pass_on(0, distance, chunk)

                @pl.when(i == 0)
                def _():
                    load_wq.wait()

                project(i)

            @pl.when(i == 1)
            def _():
                load_wo.wait()

            @pl.when(i > 0)
            def _():
                update(i - 1)

            @pl.when(i == 0)
            def _():
                load_cache.wait()

            @pl.when(i < MICRO)
            def _():
                attend_rows(i)
                attended_copy(i, own_rows).start()

                @pl.when(i >= half)
                def _():
                    branch_copy(i, own_rows).start()

            return carry

        lax.fori_loop(0, MICRO + 1, step, 0)
        for chunk in range(CHUNKS):
            pass_on(0, chips - 1, chunk)
        gathered(0)

        def finish(i, carry):
            branch_copy(i, own_rows).wait_recv()
            corner_copy(i, other_rows).wait_recv()
            added(
                att_in[i],
                wx,
                ready.at[i],
                depths(i) > 1,
                out.at[token_rows(i)],
                0,
                span,
                0,
                0,
            )
            return carry

        lax.fori_loop(0, MICRO, finish, 0)

        def drain(i, carry):
            partial_copy(i).wait_send()
            attended_copy(i, own_rows).wait_send()

            @pl.when(i < half)
            def _():
                low_copy(i, span).wait_send()
                high_copy(i).wait_send()

            @pl.when(i >= half)
            def _():
                branch_copy(i, own_rows).wait_send()
                if low:
                    low_copy(i, low).wait_send()

            return carry

        lax.fori_loop(0, MICRO, drain, 0)
        settle_weights(0)

    def second_layer():
        hidden_copy(0).start()
        for chunk in range(CHUNKS):
            weight_out(1, chunk).start()
        for i in range(1, half):
            hidden_copy(i).start()
        for i in range(half):
            rest_copy(i).start()
        load_wo.start()
        load_wq.wait()
        load_cache.wait()
        for chunk in range(CHUNKS):
            spread(1, chunk)

        def relay(i):
            branch_copy(i, own_rows).wait_recv()
            relay_copy(i, own_rows).start()

        def early(i):
            high_copy(i).wait_recv()
            low_copy(i, span).wait_recv()
            project(i)

        def late(i):
            rest_copy(i - half).wait()
            relay_copy(i, other_rows).wait_recv()
            added(
                att_in[i],
                wx,
                stage.at[i],
                depths(i) > 0,
                stage.at[i],
                low,
                width,
                -low,
                0,
            )
            total = scale(i, low, width)
            multiply(low, width, False)
            if low:
                low_copy(i, low).wait_recv()
                total = total + scale(i, 0, low)
                multiply(0, low, True)
            squares[...] = jnp.broadcast_to(total, squares.shape)
            send_partial(i)

        def update(i):
            attended_copy(i, other_rows).wait_recv()
            added(
                att[i],
                wo,
                stage.at[i],
                depths(i) > 1,
                out.at[token_rows(i)],
                span,
                width,
                0,
                -span,
            )

        def step(i, carry):
            for distance in range(1, chips):

                @pl.when(i == min(distance - 1, half - 1))
                def _():
                    for chunk in range(CHUNKS):
                        pass_on(1, distance, chunk)

            @pl.when(i < half)
            def _():
                early(i)

            @pl.when(i == half)
            def _():
                gathered(1)
                relay(half)

            @pl.when((i >= half) & (i < MICRO))
            def _():
                late(i)

            @pl.when((i >= half) & (i < MICRO - 1))
            def _():
                relay(i + 1)

            @pl.when(i == 1)
            def _():
                load_wo.wait()

            @pl.when(i > 0)
            def _():
                update(i - 1)

            @pl.when(i < MICRO)
            def _():
                attend_rows(i)
                corner_copy(i, own_rows).start()
                branch_copy(i, own_rows).start()
                attended_copy(i, own_rows).start()

            return carry

        lax.fori_loop(0, MICRO + 1, step, 0)

        def drain(i, carry):
            partial_copy(i).wait_send()
            attended_copy(i, own_rows).wait_send()
            branch_copy(i, own_rows).wait_send()
            corner_copy(i, own_rows).wait_send()

            @pl.when(i < half)
            def _():
                hidden_copy(i).wait_send()

            @pl.when(i >= half)
            def _():
                relay_copy(i, own_rows).wait_send()

            return carry

        lax.fori_loop(0, MICRO, drain, 0)
        settle_weights(1)

    @pl.when(seg == 0)
    def _():
        first_layer()

    @pl.when(seg == 1)
    def _():
        second_layer()


def cycle_of_two(chips, hidden, exit_layer, lengths, kv_cache, norm_gain, w_qkv, w_out):
    shards = 2
    width = w_qkv.shape[1]
    columns = w_qkv.shape[2]
    query_width = w_out.shape[1]
    head_size = (columns - query_width) // 2
    heads = query_width // head_size
    rows = BLOCK // shards
    span = width // 2
    wide = span + span // 2
    tokens = exit_layer.shape[0]
    hbm = pl.BlockSpec(memory_space=pltpu.HBM)
    vmem = pl.BlockSpec(memory_space=pltpu.VMEM)
    dma = pltpu.SemaphoreType.DMA((MICRO,))
    pieces = pltpu.SemaphoreType.DMA((chips, CHUNKS))
    bf16 = jnp.bfloat16
    return pl.pallas_call(
        functools.partial(cycle_kernel, (shards, head_size, heads)),
        out_shape=pltpu.VMEM((MICRO * BLOCK, span), bf16),
        in_specs=[hbm, vmem, vmem, hbm, vmem, hbm, hbm],
        out_specs=vmem,
        scratch_shapes=[
            pltpu.VMEM(w_qkv.shape[1:], bf16),
            pltpu.VMEM(w_out.shape[1:], bf16),
            pltpu.VMEM(kv_cache.shape[1:], bf16),
            pltpu.VMEM((MICRO, BLOCK, width), bf16),
            pltpu.VMEM((MICRO, BLOCK, width), bf16),
            pltpu.VMEM((MICRO * BLOCK, 128), jnp.int32),
            pltpu.VMEM((BLOCK, width), bf16),
            pltpu.VMEM((BLOCK, columns), jnp.float32),
            pltpu.VMEM((BLOCK, 128), jnp.float32),
            pltpu.VMEM((MICRO, rows, columns + 256), bf16),
            pltpu.VMEM((MICRO, rows, columns + 256), bf16),
            pltpu.VMEM((MICRO, BLOCK, query_width), bf16),
            pltpu.VMEM((query_width, wide), bf16),
            pltpu.VMEM((MICRO, BLOCK, query_width), bf16),
            pltpu.SemaphoreType.DMA((3,)),
            dma,
            pltpu.SemaphoreType.DMA((CHUNKS,)),
            pltpu.SemaphoreType.DMA((CHUNKS,)),
        ]
        + [pieces] * 6
        + [dma] * 16,
        compiler_params=pltpu.CompilerParams(
            collective_id=0, has_side_effects=True, vmem_limit_bytes=VMEM_LIMIT
        ),
        name="cycle",
    )(
        hidden[0],
        exit_layer.reshape(1, tokens),
        lengths.reshape(1, tokens),
        kv_cache[0],
        norm_gain,
        w_qkv[0],
        w_out[0],
    )


def chosen(batches, devices, *arguments):
    shards = max(2, devices // 4)
    if shards == 2 and devices // shards == 2:
        return cycle_of_two(batches // 2, *arguments)
    return body(*arguments)


def solution(mesh):
    return jax.shard_map(
        functools.partial(chosen, mesh.shape["blk"], mesh.shape["section"]),
        mesh=mesh,
        in_specs=(
            P("section", "blk", None),
            P("blk"),
            P("blk"),
            P("section", "blk", None, None),
            P("section", None),
            P("section", None, None),
            P("section", None, None),
        ),
        out_specs=P("blk", "section"),
        check_vma=False,
    )
```

time: 120 us -> 127 us (1.058)
  Pallas kernels: 115 us -> 125 us
  local copies, waits for them, and re-layouts: 4.02 us -> 1.32 us
    pallas_call x1, Pallas kernels: 115 us -> 125 us  [cycle_of_two(): pl.pallas_call(functools.partial(cycle_kernel, (shards, head_size, heads)...]
    unnamed x1, local copies, waits for them, and re-layouts: 3.16 us -> 1.32 us
where the time goes in v1:
time: 127 us; the launch traced here: 126 us
  Pallas kernels  125 us (98%)
  local copies, waits for them, and re-layouts  1.32 us (1%)
    pallas_call x1, Pallas kernels, cycle_of_two(): pl.pallas_call(functools.partial(cycle_kernel, (shards, head_size, heads)...  125 us

profile of v1, /device:TPU:0, one launch (start us, length us, event | category | flops | bytes accessed | tf_op | source)
XLA Modules:
  0.0 126.5 jit_solution(17999389543776578729)
XLA Ops:
  0.0 125.2 %cycle.1 = bf16[512,2048]{1,0:T(8,128)(2,1)S(1)} custom-call(bf16[256,4096]{1,0:T(8,128)(2,1)} %bitcast.8, s32[1,512]{1,0:T(1,128)} %bitcast.10, s32[1,512]{1,0:T(1,128)} %bitcast.11, bf16[256,16,256]{2,1,0:T(8,128)(2,1)} %bitcast.9, bf16[1,4096]{1,0:T(2,128)(2,1)} %gain.1, bf16[4096,1280]{1,0:T(8,128)(2,1)} %bitcast.6, bf16[1024,4096]{1,0:T(8,128)(2,1)} %bitcast.7), custom_call_target="tpu_custom_call" | custom-call | tf_op jit(solution)/shard_map/cycle/pallas_call | solution.py:860
  125.2 1.3 %copy.9 = bf16[512,2048]{1,0:T(8,128)(2,1)} copy(bf16[512,2048]{1,0:T(8,128)(2,1)S(1)} %cycle.1) | data formatting | bytes 4194304

commit v2 on v1

--- a/solution.py
+++ b/solution.py
@@ -380,26 +380,51 @@
 
         sideways(layer, chip, chunk, core).start()
 
+    def from_below(layer, distance, chunk):
+        owner = chip - distance
+
+        @pl.when(owner >= 0)
+        def _():
+            upward(layer, owner, chunk).wait_recv()
+
+            @pl.when(has_above)
+            def _():
+                upward(layer, owner, chunk).start()
+
+            sideways(layer, owner, chunk, core).start()
+
+    def from_above(layer, distance, chunk):
+        owner = chip + distance
+
+        @pl.when(owner < chips)
+        def _():
+            downward(layer, owner, chunk).wait_recv()
+
+            @pl.when(has_below)
+            def _():
+                downward(layer, owner, chunk).start()
+
+            sideways(layer, owner, chunk, core).start()
+
     def pass_on(layer, distance, chunk):
-        @pl.when(chip >= distance)
+        @pl.when(has_above)
         def _():
-            upward(layer, chip - distance, chunk).wait_recv()
-
-            @pl.when(has_above)
-            def _():
-                upward(layer, chip - distance, chunk).start()
-
-            sideways(layer, chip - distance, chunk, core).start()
-
-        @pl.when(chip + distance < chips)
+            from_below(layer, distance, chunk)
+
+        @pl.when(has_below)
         def _():
-            downward(layer, chip + distance, chunk).wait_recv()
-
-            @pl.when(has_below)
-            def _():
-                downward(layer, chip + distance, chunk).start()
-
-            sideways(layer, chip + distance, chunk, core).start()
+            from_above(layer, distance, chunk)
+
+    def collect(layer, chunk):
+        for distance in range(1, chips):
+
+            @pl.when(jnp.logical_not(has_above))
+            def _():
+                from_below(layer, distance, chunk)
+
+            @pl.when(jnp.logical_not(has_below))
+            def _():
+                from_above(layer, distance, chunk)
 
     def gathered(layer):
         for owner in range(chips):
@@ -488,6 +513,11 @@
             a_recv.at[i],
             {"section": across},
         )
+
+    def turn(layer, t):
+        last = half if layer == 0 else MICRO - 1
+        moved = jnp.where((t >= half - 1) & (t < last), t + 1, t)
+        return jnp.where(t == last, half - 1, moved)
 
     def scale(i, first, last):
         total = jnp.zeros((BLOCK, 1), jnp.float32)
@@ -499,7 +529,7 @@
             scaled[:, cols] = (piece * gain[:, cols].astype(jnp.float32)).astype(jnp.bfloat16)
         return total
 
-    def multiply(first, last, more):
+    def multiply(slot, first, last, more):
         step = 512
         for start in range(0, columns, step):
             cols = pl.ds(start, min(step, columns - start))
@@ -508,30 +538,35 @@
                 wq[pl.ds(first, last - first), cols],
                 preferred_element_type=jnp.float32,
             )
-            partial[:, cols] = partial[:, cols] + product if more else product
-
-    def send_partial(i):
-        psend[i, :, pl.ds(0, columns)] = partial[other_rows, :].astype(jnp.bfloat16)
-        theirs = squares[other_rows, :]
+            if more:
+                product = partial[slot, :, cols] + product
+            partial[slot, :, cols] = product
+
+    def send_partial(i, slot):
+        psend[i, :, pl.ds(0, columns)] = partial[slot, other_rows, :].astype(jnp.bfloat16)
+        theirs = squares[slot, other_rows, :]
         coarse = theirs.astype(jnp.bfloat16)
         fine = (theirs - coarse.astype(jnp.float32)).astype(jnp.bfloat16)
         psend[i, :, pl.ds(columns, 128)] = coarse
         psend[i, :, pl.ds(columns + 128, 128)] = fine
         partial_copy(i).start()
 
-    def project(i):
-        squares[...] = jnp.broadcast_to(scale(i, 0, width), squares.shape)
-        multiply(0, width, False)
-        send_partial(i)
-
-    def attend_rows(i):
+    def keep_squares(slot, total):
+        squares[slot] = jnp.broadcast_to(total, squares.shape[1:])
+
+    def project(i, slot):
+        keep_squares(slot, scale(i, 0, width))
+        multiply(slot, 0, width, False)
+        send_partial(i, slot)
+
+    def attend_rows(i, slot):
         partial_copy(i).wait_recv()
         coarse = precv[i, :, pl.ds(columns, 128)].astype(jnp.float32)
         fine = precv[i, :, pl.ds(columns + 128, 128)].astype(jnp.float32)
-        total_squares = squares[own_rows, :] + coarse + fine
+        total_squares = squares[slot, own_rows, :] + coarse + fine
         factor = lax.rsqrt(total_squares / (width * shards) + EPSILON)[:, :1]
         fitted = (
-            partial[own_rows, :] + precv[i, :, pl.ds(0, columns)].astype(jnp.float32)
+            partial[slot, own_rows, :] + precv[i, :, pl.ds(0, columns)].astype(jnp.float32)
         ) * factor
         scale = 1.0 / math.sqrt(head_size)
         query = jnp.concatenate(
@@ -585,9 +620,8 @@
                 chosen, kept + branch, kept
             ).astype(jnp.bfloat16)
 
-    pl.semaphore_wait(
-        barrier, 4 + has_above.astype(jnp.int32) + has_below.astype(jnp.int32)
-    )
+    neighbours = has_above.astype(jnp.int32) + has_below.astype(jnp.int32)
+    pl.semaphore_wait(barrier, 4 + neighbours)
 
     def first_layer():
         for chunk in range(CHUNKS):
@@ -602,10 +636,16 @@
             fill = functools.partial(added, att[i], wo, stage.at[i], active, ready.at[i])
             fill(0, span, 0, 0)
 
+            @pl.when(i < half - 1)
+            def _():
+                low_copy(i, span).start()
+
             @pl.when(i < half)
             def _():
-                low_copy(i, span).start()
                 fill(span, width, 0, 0)
+
+            @pl.when(i < half - 1)
+            def _():
                 high_copy(i).start()
 
             if low:
@@ -614,64 +654,78 @@
                 def _():
                     low_copy(i, low).start()
 
-        def step(i, carry):
-            @pl.when(i < MICRO)
-            def _():
-                @pl.when(i < half)
+            @pl.when(i == MICRO - 1)
+            def _():
+                low_copy(half - 1, span).start()
+                high_copy(half - 1).start()
+
+        def step(t, carry):
+            i = turn(0, t)
+
+            @pl.when(i < half)
+            def _():
+                own_copy(i).wait()
+
+            @pl.when(i >= half)
+            def _():
+                hidden_copy(i - half).wait_recv()
+
+            @pl.when(t == half - 1)
+            def _():
+                spread(0, 0)
+
+            for distance in range(1, chips - 1):
+
+                @pl.when(t == min(half + distance, MICRO - 1))
                 def _():
-                    own_copy(i).wait()
-
-                @pl.when(i == half)
-                def _():
-                    for chunk in range(CHUNKS):
-                        spread(0, chunk)
-
-                @pl.when(i >= half)
-                def _():
-                    hidden_copy(i - half).wait_recv()
-
-                for distance in range(1, chips - 1):
-
-                    @pl.when(i == half + 1 + distance)
-                    def _():
-                        for chunk in range(CHUNKS):
-                            pass_on(0, distance, chunk)
-
-                @pl.when(i == 0)
-                def _():
-                    load_wq.wait()
-
-                project(i)
-
-            @pl.when(i == 1)
+                    pass_on(0, distance, 0)
+
+            @pl.when(t == 0)
+            def _():
+                load_wq.wait()
+
+            project(i, 0)
+
+            @pl.when(t == 1)
             def _():
                 load_wo.wait()
 
-            @pl.when(i > 0)
-            def _():
-                update(i - 1)
-
-            @pl.when(i == 0)
+            @pl.when((t > 0) & (t < MICRO - 1))
+            def _():
+                update(turn(0, t - 1))
+
+            @pl.when(t == 0)
             def _():
                 load_cache.wait()
 
-            @pl.when(i < MICRO)
-            def _():
-                attend_rows(i)
-                attended_copy(i, own_rows).start()
-
-                @pl.when(i >= half)
-                def _():
-                    branch_copy(i, own_rows).start()
+            attend_rows(i, 0)
+
+            @pl.when(i >= half)
+            def _():
+                branch_copy(i, own_rows).start()
+
+            attended_copy(i, own_rows).start()
+
+            @pl.when(t >= MICRO - 2)
+            def _():
+                update(i)
 
             return carry
 
-        lax.fori_loop(0, MICRO + 1, step, 0)
-        for chunk in range(CHUNKS):
-            pass_on(0, chips - 1, chunk)
+        lax.fori_loop(0, MICRO, step, 0)
+        pass_on(0, chips - 1, 0)
+        collect(0, 0)
+        for chunk in range(1, CHUNKS):
+            spread(0, chunk)
+        for distance in range(1, chips):
+            for chunk in range(1, CHUNKS):
+                pass_on(0, distance, chunk)
+        for chunk in range(1, CHUNKS):
+            collect(0, chunk)
         gathered(0)
 
-        def finish(i, carry):
+        def finish(t, carry):
+            i = turn(1, t)
             branch_copy(i, own_rows).wait_recv()
             corner_copy(i, other_rows).wait_recv()
             added(
@@ -711,10 +765,11 @@
 
     def second_layer():
         hidden_copy(0).start()
-        for chunk in range(CHUNKS):
-            weight_out(1, chunk).start()
+        weight_out(1, 0).start()
         for i in range(1, half):
             hidden_copy(i).start()
+        for chunk in range(1, CHUNKS):
+            weight_out(1, chunk).start()
         for i in range(half):
             rest_copy(i).start()
         load_wo.start()
@@ -727,13 +782,22 @@
             branch_copy(i, own_rows).wait_recv()
             relay_copy(i, own_rows).start()
 
-        def early(i):
+        def early(i, slot):
+            low_copy(i, span).wait_recv()
+            total = scale(i, 0, span)
+            multiply(slot, 0, span, False)
             high_copy(i).wait_recv()
-            low_copy(i, span).wait_recv()
-            project(i)
-
-        def late(i):
-            rest_copy(i - half).wait()
+            total = total + scale(i, span, width)
+            multiply(slot, span, width, True)
+
+            @pl.when(i == half - 2)
+            def _():
+                relay(half)
+
+            keep_squares(slot, total)
+            send_partial(i, slot)
+
+        def late(i, slot):
             relay_copy(i, other_rows).wait_recv()
             added(
                 att_in[i],
@@ -746,14 +810,19 @@
                 -low,
                 0,
             )
+
+            @pl.when(i < MICRO - 1)
+            def _():
+                relay(i + 1)
+
             total = scale(i, low, width)
-            multiply(low, width, False)
+            multiply(slot, low, width, False)
             if low:
                 low_copy(i, low).wait_recv()
                 total = total + scale(i, 0, low)
-                multiply(0, low, True)
-            squares[...] = jnp.broadcast_to(total, squares.shape)
-            send_partial(i)
+                multiply(slot, 0, low, True)
+            keep_squares(slot, total)
+            send_partial(i, slot)
 
         def update(i):
             attended_copy(i, other_rows).wait_recv()
@@ -769,49 +838,59 @@
                 -span,
             )
 
-        def step(i, carry):
+        def step(t, carry):
+            i = turn(1, t)
+
             for distance in range(1, chips):
 
-                @pl.when(i == min(distance - 1, half - 1))
+                @pl.when(t == min(distance - 1, half - 1))
                 def _():
                     for chunk in range(CHUNKS):
                         pass_on(1, distance, chunk)
 
             @pl.when(i < half)
             def _():
-                early(i)
-
-            @pl.when(i == half)
-            def _():
+                early(i, t % 2)
+
+            @pl.when(t == half - 1)
+            def _():
+                for chunk in range(CHUNKS):
+                    collect(1, chunk)
                 gathered(1)
-                relay(half)
-
-            @pl.when((i >= half) & (i < MICRO))
-            def _():
-                late(i)
-
-            @pl.when((i >= half) & (i < MICRO - 1))
-            def _():
-                relay(i + 1)
-
-            @pl.when(i == 1)
+                for j in range(half):
+                    rest_copy(j).wait()
+
+            @pl.when((i >= half) & (t < MICRO))
+            def _():
+                late(i, t % 2)
+
+            @pl.when(t == MICRO)
+            def _():
+                update(half)
+                update(half + 1)
+                update(half + 2)
+
+            @pl.when(t > 0)
+            def _():
+                j = turn(1, t - 1)
+                attend_rows(j, (t - 1) % 2)
+                corner_copy(j, own_rows).start()
+                branch_copy(j, own_rows).start()
+                attended_copy(j, own_rows).start()
+
+            @pl.when(t == 1)
             def _():
                 load_wo.wait()
 
-            @pl.when(i > 0)
-            def _():
-                update(i - 1)
-
-            @pl.when(i < MICRO)
-            def _():
-                attend_rows(i)
-                corner_copy(i, own_rows).start()
-                branch_copy(i, own_rows).start()
-                attended_copy(i, own_rows).start()
+            @pl.when((t > 1) & (t < half + 1))
+            def _():
+                update(turn(1, t - 2))
 
             return carry
 
         lax.fori_loop(0, MICRO + 1, step, 0)
+        update(MICRO - 1)
+        update(half - 1)
 
         def drain(i, carry):
             partial_copy(i).wait_send()
@@ -870,8 +949,8 @@
             pltpu.VMEM((MICRO, BLOCK, width), bf16),
             pltpu.VMEM((MICRO * BLOCK, 128), jnp.int32),
             pltpu.VMEM((BLOCK, width), bf16),
-            pltpu.VMEM((BLOCK, columns), jnp.float32),
-            pltpu.VMEM((BLOCK, 128), jnp.float32),
+            pltpu.VMEM((2, BLOCK, columns), jnp.float32),
+            pltpu.VMEM((2, BLOCK, 128), jnp.float32),
             pltpu.VMEM((MICRO, rows, columns + 256), bf16),
             pltpu.VMEM((MICRO, rows, columns + 256), bf16),
             pltpu.VMEM((MICRO, BLOCK, query_width), bf16),

time: 127 us -> 107 us (0.84)
  Pallas kernels: 125 us -> 104 us
    pallas_call x1, Pallas kernels: 125 us -> 104 us  [cycle_of_two(): pl.pallas_call(functools.partial(cycle_kernel, (shards, head_size, heads)...]
where the time goes in v2:
time: 107 us; the launch traced here: 106 us
  Pallas kernels  104 us (97%)
  local copies, waits for them, and re-layouts  1.32 us (1%)
    pallas_call x1, Pallas kernels, cycle_of_two(): pl.pallas_call(functools.partial(cycle_kernel, (shards, head_size, heads)...  104 us

profile of v2, /device:TPU:0, one launch (start us, length us, event | category | flops | bytes accessed | tf_op | source)
XLA Modules:
  0.0 105.7 jit_solution(10594194269988546119)
XLA Ops:
  0.0 104.4 %cycle.1 = bf16[512,2048]{1,0:T(8,128)(2,1)S(1)} custom-call(bf16[256,4096]{1,0:T(8,128)(2,1)} %bitcast.8, s32[1,512]{1,0:T(1,128)} %bitcast.10, s32[1,512]{1,0:T(1,128)} %bitcast.11, bf16[256,16,256]{2,1,0:T(8,128)(2,1)} %bitcast.9, bf16[1,4096]{1,0:T(2,128)(2,1)} %gain.1, bf16[4096,1280]{1,0:T(8,128)(2,1)} %bitcast.6, bf16[1024,4096]{1,0:T(8,128)(2,1)} %bitcast.7), custom_call_target="tpu_custom_call" | custom-call | tf_op jit(solution)/shard_map/cycle/pallas_call | solution.py:939
  104.4 1.3 %copy.9 = bf16[512,2048]{1,0:T(8,128)(2,1)} copy(bf16[512,2048]{1,0:T(8,128)(2,1)S(1)} %cycle.1) | data formatting | bytes 4194304

commit v3 on v2

--- a/solution.py
+++ b/solution.py
@@ -179,7 +179,8 @@
 
 
 MESH = pl.DeviceIdType.MESH
-CHUNKS = 2
+CHUNKS = 4
+EARLY = 3
 
 
 def cycle_kernel(
@@ -319,6 +320,8 @@
         table[cols, :] = jnp.where(lane == 0, depth, limit)
 
     def place(i):
+        if isinstance(i, int):
+            return 2 * i if i < half else 2 * (i - half) + 1
         return jnp.where(i < half, 2 * i, 2 * (i - half) + 1)
 
     def token_rows(i):
@@ -500,6 +503,10 @@
             {"section": across},
         )
 
+    def relay(i):
+        branch_copy(i, own_rows).wait_recv()
+        relay_copy(i, own_rows).start()
+
     def partial_copy(i):
         return remote(
             psend.at[i], precv.at[i], p_send.at[i], p_recv.at[i], {"section": across}
@@ -519,52 +526,58 @@
         moved = jnp.where((t >= half - 1) & (t < last), t + 1, t)
         return jnp.where(t == last, half - 1, moved)
 
-    def scale(i, first, last):
-        total = jnp.zeros((BLOCK, 1), jnp.float32)
-        size = min(last - first, 512)
-        for start in range(first, last, size):
-            cols = pl.ds(start, size)
-            piece = stage[i, :, cols].astype(jnp.float32)
+    def blocks_at(ref, i, count, cols):
+        return ref[pl.ds(i, count), :, cols].reshape(count * BLOCK, cols.size)
+
+    def scale(i, count, first, last):
+        total = jnp.zeros((count * BLOCK, 1), jnp.float32)
+        for start in range(first, last, 512):
+            cols = pl.ds(start, min(512, last - start))
+            piece = blocks_at(stage, i, count, cols).astype(jnp.float32)
             total = total + jnp.sum(piece * piece, axis=1, keepdims=True)
-            scaled[:, cols] = (piece * gain[:, cols].astype(jnp.float32)).astype(jnp.bfloat16)
+            scaled[pl.ds(0, count * BLOCK), cols] = (
+                piece * gain[:, cols].astype(jnp.float32)
+            ).astype(jnp.bfloat16)
         return total
 
-    def multiply(slot, first, last, more):
+    def multiply(slot, count, first, last, more):
         step = 512
         for start in range(0, columns, step):
             cols = pl.ds(start, min(step, columns - start))
             product = jnp.dot(
-                scaled[:, pl.ds(first, last - first)],
+                scaled[pl.ds(0, count * BLOCK), pl.ds(first, last - first)],
                 wq[pl.ds(first, last - first), cols],
                 preferred_element_type=jnp.float32,
             )
             if more:
-                product = partial[slot, :, cols] + product
-            partial[slot, :, cols] = product
+                product = blocks_at(partial, slot, count, cols) + product
+            partial[pl.ds(slot, count), :, cols] = product.reshape(count, BLOCK, cols.size)
 
     def send_partial(i, slot):
         psend[i, :, pl.ds(0, columns)] = partial[slot, other_rows, :].astype(jnp.bfloat16)
         theirs = squares[slot, other_rows, :]
         coarse = theirs.astype(jnp.bfloat16)
         fine = (theirs - coarse.astype(jnp.float32)).astype(jnp.bfloat16)
-        psend[i, :, pl.ds(columns, 128)] = coarse
-        psend[i, :, pl.ds(columns + 128, 128)] = fine
+        first = lax.broadcasted_iota(jnp.int32, theirs.shape, 1) == 0
+        psend[i, :, pl.ds(columns, 128)] = jnp.where(
+            first, coarse.astype(jnp.float32), fine.astype(jnp.float32)
+        ).astype(jnp.bfloat16)
         partial_copy(i).start()
 
-    def keep_squares(slot, total):
-        squares[slot] = jnp.broadcast_to(total, squares.shape[1:])
+    def keep_squares(slot, count, total):
+        spread_out = jnp.broadcast_to(total, (count * BLOCK, 128))
+        squares[pl.ds(slot, count)] = spread_out.reshape(count, BLOCK, 128)
 
     def project(i, slot):
-        keep_squares(slot, scale(i, 0, width))
-        multiply(slot, 0, width, False)
+        keep_squares(slot, 1, scale(i, 1, 0, width))
+        multiply(slot, 1, 0, width, False)
         send_partial(i, slot)
 
     def attend_rows(i, slot):
         partial_copy(i).wait_recv()
-        coarse = precv[i, :, pl.ds(columns, 128)].astype(jnp.float32)
-        fine = precv[i, :, pl.ds(columns + 128, 128)].astype(jnp.float32)
-        total_squares = squares[slot, own_rows, :] + coarse + fine
-        factor = lax.rsqrt(total_squares / (width * shards) + EPSILON)[:, :1]
+        theirs = precv[i, :, pl.ds(columns, 128)].astype(jnp.float32)
+        total_squares = squares[slot, own_rows, :][:, :1] + (theirs[:, :1] + theirs[:, 1:2])
+        factor = lax.rsqrt(total_squares / (width * shards) + EPSILON)
         fitted = (
             partial[slot, own_rows, :] + precv[i, :, pl.ds(0, columns)].astype(jnp.float32)
         ) * factor
@@ -608,8 +621,8 @@
         )
 
     def added(source, weight, before, chosen, target, first, last, shift_weight, shift):
-        size = min(last - first, 512)
-        for start in range(first, last, size):
+        for start in range(first, last, 512):
+            size = min(512, last - start)
             branch = jnp.dot(
                 source,
                 weight[:, pl.ds(start + shift_weight, size)],
@@ -636,7 +649,7 @@
             fill = functools.partial(added, att[i], wo, stage.at[i], active, ready.at[i])
             fill(0, span, 0, 0)
 
-            @pl.when(i < half - 1)
+            @pl.when(i < half - 2)
             def _():
                 low_copy(i, span).start()
 
@@ -644,7 +657,7 @@
             def _():
                 fill(span, width, 0, 0)
 
-            @pl.when(i < half - 1)
+            @pl.when(i < half - 2)
             def _():
                 high_copy(i).start()
 
@@ -672,13 +685,15 @@
 
             @pl.when(t == half - 1)
             def _():
-                spread(0, 0)
+                for chunk in range(EARLY):
+                    spread(0, chunk)
 
             for distance in range(1, chips - 1):
 
                 @pl.when(t == min(half + distance, MICRO - 1))
                 def _():
-                    pass_on(0, distance, 0)
+                    for chunk in range(EARLY):
+                        pass_on(0, distance, chunk)
 
             @pl.when(t == 0)
             def _():
@@ -686,6 +701,11 @@
 
             project(i, 0)
 
+            @pl.when(t == MICRO - 1)
+            def _():
+                for chunk in range(EARLY, CHUNKS):
+                    spread(0, chunk)
+
             @pl.when(t == 1)
             def _():
                 load_wo.wait()
@@ -704,8 +724,21 @@
             def _():
                 branch_copy(i, own_rows).start()
 
+            @pl.when(i == half + 1)
+            def _():
+                low_copy(half - 2, span).start()
+
+            @pl.when(i == half + 2)
+            def _():
+                high_copy(half - 2).start()
+
             attended_copy(i, own_rows).start()
 
+            @pl.when(t == MICRO - 1)
+            def _():
+                for chunk in range(EARLY, CHUNKS):
+                    pass_on(0, 1, chunk)
+
             @pl.when(t >= MICRO - 2)
             def _():
                 update(i)
@@ -713,35 +746,36 @@
             return carry
 
         lax.fori_loop(0, MICRO, step, 0)
-        pass_on(0, chips - 1, 0)
-        collect(0, 0)
-        for chunk in range(1, CHUNKS):
-            spread(0, chunk)
-        for distance in range(1, chips):
-            for chunk in range(1, CHUNKS):
+        relay(0)
+        for chunk in range(EARLY):
+            pass_on(0, chips - 1, chunk)
+            collect(0, chunk)
+        relay(1)
+        for distance in range(2, chips):
+            for chunk in range(EARLY, CHUNKS):
                 pass_on(0, distance, chunk)
-        for chunk in range(1, CHUNKS):
+        for chunk in range(EARLY, CHUNKS):
             collect(0, chunk)
+        for i in range(2, half - 1):
+            relay(i)
         gathered(0)
 
-        def finish(t, carry):
-            i = turn(1, t)
-            branch_copy(i, own_rows).wait_recv()
-            corner_copy(i, other_rows).wait_recv()
-            added(
-                att_in[i],
-                wx,
-                ready.at[i],
-                depths(i) > 1,
-                out.at[token_rows(i)],
-                0,
-                span,
-                0,
-                0,
-            )
-            return carry
-
-        lax.fori_loop(0, MICRO, finish, 0)
+        def finish(i, count):
+            for j in range(i, i + count):
+                if j == half - 1:
+                    branch_copy(j, own_rows).wait_recv()
+                    corner_copy(j, other_rows).wait_recv()
+                else:
+                    relay_copy(j, other_rows).wait_recv()
+            source = att_in[pl.ds(i, count)].reshape(count * BLOCK, query_width)
+            deep = jnp.concatenate([depths(j) for j in range(i, i + count)], axis=0) > 1
+            for start in range(0, span, 512):
+                cols = pl.ds(start, min(512, span - start))
+                branch = jnp.dot(source, wx[:, cols], preferred_element_type=jnp.float32)
+                kept = blocks_at(ready, i, count, cols).astype(jnp.float32)
+                now = jnp.where(deep, kept + branch, kept).astype(jnp.bfloat16)
+                for j in range(count):
+                    out[token_rows(i + j), cols] = now[j * BLOCK : (j + 1) * BLOCK]
 
         def drain(i, carry):
             partial_copy(i).wait_send()
@@ -760,15 +794,35 @@
 
             return carry
 
+        def unrelay(i, carry):
+            @pl.when(i != half - 1)
+            def _():
+                relay_copy(i, own_rows).wait_send()
+
+            return carry
+
+        finish(0, 2)
+        settle_weights(0)
         lax.fori_loop(0, MICRO, drain, 0)
-        settle_weights(0)
+        relay(half)
+        relay(half + 1)
+        finish(2, 1)
+        relay(half + 2)
+        finish(half, 2)
+        relay(half + 3)
+        lax.fori_loop(0, half + 2, unrelay, 0)
+        finish(half + 2, 2)
+        finish(half - 1, 1)
+
+        lax.fori_loop(half + 2, MICRO, unrelay, 0)
 
     def second_layer():
         hidden_copy(0).start()
-        weight_out(1, 0).start()
+        for chunk in range(EARLY):
+            weight_out(1, chunk).start()
         for i in range(1, half):
             hidden_copy(i).start()
-        for chunk in range(1, CHUNKS):
+        for chunk in range(EARLY, CHUNKS):
             weight_out(1, chunk).start()
         for i in range(half):
             rest_copy(i).start()
@@ -778,51 +832,48 @@
         for chunk in range(CHUNKS):
             spread(1, chunk)
 
-        def relay(i):
-            branch_copy(i, own_rows).wait_recv()
-            relay_copy(i, own_rows).start()
-
-        def early(i, slot):
+        def first_half(i, slot):
             low_copy(i, span).wait_recv()
-            total = scale(i, 0, span)
-            multiply(slot, 0, span, False)
+            total = scale(i, 1, 0, span)
+            multiply(slot, 1, 0, span, False)
+            return total
+
+        def second_half(i, slot, total):
             high_copy(i).wait_recv()
-            total = total + scale(i, span, width)
-            multiply(slot, span, width, True)
-
-            @pl.when(i == half - 2)
-            def _():
-                relay(half)
-
-            keep_squares(slot, total)
+            total = total + scale(i, 1, span, width)
+            multiply(slot, 1, span, width, True)
+            keep_squares(slot, 1, total)
             send_partial(i, slot)
 
         def late(i, slot):
-            relay_copy(i, other_rows).wait_recv()
-            added(
-                att_in[i],
-                wx,
-                stage.at[i],
-                depths(i) > 0,
-                stage.at[i],
-                low,
-                width,
-                -low,
-                0,
-            )
-
-            @pl.when(i < MICRO - 1)
-            def _():
-                relay(i + 1)
-
-            total = scale(i, low, width)
-            multiply(slot, low, width, False)
+            for j in range(2):
+                relay_copy(i + j, other_rows).wait_recv()
+            source = att_in[pl.ds(i, 2)].reshape(2 * BLOCK, query_width)
+            active = jnp.concatenate([depths(i), depths(i + 1)], axis=0) > 0
+            for start in range(low, width, 512):
+                size = min(512, width - start)
+                cols = pl.ds(start, size)
+                branch = jnp.dot(
+                    source, wx[:, pl.ds(start - low, size)], preferred_element_type=jnp.float32
+                )
+                kept = blocks_at(stage, i, 2, cols).astype(jnp.float32)
+                now = jnp.where(active, kept + branch, kept).astype(jnp.bfloat16)
+                stage[pl.ds(i, 2), :, cols] = now.reshape(2, BLOCK, size)
+
+            @pl.when(i == half)
+            def _():
+                relay(half + 3)
+
+            total = scale(i, 2, low, width)
+            multiply(slot, 2, low, width, False)
             if low:
-                low_copy(i, low).wait_recv()
-                total = total + scale(i, 0, low)
-                multiply(slot, 0, low, True)
-            keep_squares(slot, total)
-            send_partial(i, slot)
+                for j in range(2):
+                    low_copy(i + j, low).wait_recv()
+                total = total + scale(i, 2, 0, low)
+                multiply(slot, 2, 0, low, True)
+            keep_squares(slot, 2, total)
+            for j in range(2):
+                send_partial(i + j, slot + j)
 
         def update(i):
             attended_copy(i, other_rows).wait_recv()
@@ -838,78 +889,114 @@
                 -span,
             )
 
-        def step(t, carry):
-            i = turn(1, t)
-
+        def attend(i, slot):
+            attend_rows(i, slot)
+            branch_copy(i, own_rows).start()
+            attended_copy(i, own_rows).start()
+
+        def early(t, carry):
             for distance in range(1, chips):
 
-                @pl.when(t == min(distance - 1, half - 1))
+                @pl.when(t == min(distance - 1, half - 2))
                 def _():
                     for chunk in range(CHUNKS):
                         pass_on(1, distance, chunk)
 
-            @pl.when(i < half)
-            def _():
-                early(i, t % 2)
-
-            @pl.when(t == half - 1)
-            def _():
+            @pl.when(t == half - 2)
+            def _():
+                for j in range(2):
+                    relay(half + j)
+
+            total = first_half(t, t % 2)
+
+            @pl.when(t == half - 2)
+            def _():
+                relay(half + 2)
                 for chunk in range(CHUNKS):
                     collect(1, chunk)
-                gathered(1)
-                for j in range(half):
-                    rest_copy(j).wait()
-
-            @pl.when((i >= half) & (t < MICRO))
-            def _():
-                late(i, t % 2)
-
-            @pl.when(t == MICRO)
-            def _():
-                update(half)
-                update(half + 1)
-                update(half + 2)
+
+            second_half(t, t % 2, total)
 
             @pl.when(t > 0)
             def _():
-                j = turn(1, t - 1)
-                attend_rows(j, (t - 1) % 2)
-                corner_copy(j, own_rows).start()
-                branch_copy(j, own_rows).start()
-                attended_copy(j, own_rows).start()
-
-            @pl.when(t == 1)
-            def _():
-                load_wo.wait()
-
-            @pl.when((t > 1) & (t < half + 1))
-            def _():
-                update(turn(1, t - 2))
+                attend(t - 1, (t - 1) % 2)
 
             return carry
 
-        lax.fori_loop(0, MICRO + 1, step, 0)
-        update(MICRO - 1)
-        update(half - 1)
+        lax.fori_loop(0, half - 1, early, 0)
+        load_wo.wait()
+        update(0)
+        gathered(1)
+        for i in range(half):
+            rest_copy(i).wait()
+
+        def pair(t, carry):
+            late(half + 2 * t, 2 - 2 * t)
+
+            @pl.when(t == 0)
+            def _():
+                attend(half - 2, (half - 2) % 2)
+                update(1)
+
+            return carry
+
+        lax.fori_loop(0, half // 2, pair, 0)
+        total = first_half(half - 1, 4)
+
+        def last(t, carry):
+            i = jnp.where(t < half, half + t, half - 1)
+
+            @pl.when(t == 2)
+            def _():
+                second_half(half - 1, 4, total)
+                for j in range(half, half + 2):
+                    attended_copy(j, own_rows).start()
+
+            attend_rows(i, jnp.where(t < half, (t + 2) % 4, 4))
+
+            @pl.when(t == half)
+            def _():
+                corner_copy(i, own_rows).start()
+
+            branch_copy(i, own_rows).start()
+
+            @pl.when(t == half - 1)
+            def _():
+                update(half - 2)
+
+            return carry
+
+        lax.fori_loop(0, half + 1, last, 0)
+        for j in (half + 2, half + 3, half - 1):
+            attended_copy(j, own_rows).start()
+        settle_weights(1)
 
         def drain(i, carry):
             partial_copy(i).wait_send()
+            branch_copy(i, own_rows).wait_send()
+
+            @pl.when(i < half)
+            def _():
+                hidden_copy(i).wait_send()
+
+            @pl.when(i >= half)
+            def _():
+                relay_copy(i, own_rows).wait_send()
+
+            return carry
+
+        lax.fori_loop(0, MICRO, drain, 0)
+
+        def settle(i, carry):
+            update(i)
             attended_copy(i, own_rows).wait_send()
-            branch_copy(i, own_rows).wait_send()
-            corner_copy(i, own_rows).wait_send()
-
-            @pl.when(i < half)
-            def _():
-                hidden_copy(i).wait_send()
-
-            @pl.when(i >= half)
-            def _():
-                relay_copy(i, own_rows).wait_send()
-
             return carry
 
-        lax.fori_loop(0, MICRO, drain, 0)
-        settle_weights(1)
+        lax.fori_loop(half, MICRO, settle, 0)
+        settle(half - 1, 0)
+        for i in range(half - 1):
+            attended_copy(i, own_rows).wait_send()
+        corner_copy(half - 1, own_rows).wait_send()
 
     @pl.when(seg == 0)
     def _():
@@ -929,7 +1016,7 @@
     heads = query_width // head_size
     rows = BLOCK // shards
     span = width // 2
-    wide = span + span // 2
+    wide = span + span * 5 // 8
     tokens = exit_layer.shape[0]
     hbm = pl.BlockSpec(memory_space=pltpu.HBM)
     vmem = pl.BlockSpec(memory_space=pltpu.VMEM)
@@ -948,11 +1035,11 @@
             pltpu.VMEM((MICRO, BLOCK, width), bf16),
             pltpu.VMEM((MICRO, BLOCK, width), bf16),
             pltpu.VMEM((MICRO * BLOCK, 128), jnp.int32),
-            pltpu.VMEM((BLOCK, width), bf16),
-            pltpu.VMEM((2, BLOCK, columns), jnp.float32),
-            pltpu.VMEM((2, BLOCK, 128), jnp.float32),
-            pltpu.VMEM((MICRO, rows, columns + 256), bf16),
-            pltpu.VMEM((MICRO, rows, columns + 256), bf16),
+            pltpu.VMEM((2 * BLOCK, width), bf16),
+            pltpu.VMEM((5, BLOCK, columns), jnp.float32),
+            pltpu.VMEM((5, BLOCK, 128), jnp.float32),
+            pltpu.VMEM((MICRO, rows, columns + 128), bf16),
+            pltpu.VMEM((MICRO, rows, columns + 128), bf16),
             pltpu.VMEM((MICRO, BLOCK, query_width), bf16),
             pltpu.VMEM((query_width, wide), bf16),
             pltpu.VMEM((MICRO, BLOCK, query_width), bf16),

time: 107 us -> 101 us (0.944); the launches traced: 106 us -> 101 us
  Pallas kernels: 104 us -> 99.5 us
    pallas_call x1, Pallas kernels: 104 us -> 99.5 us  [cycle_of_two(): pl.pallas_call(functools.partial(cycle_kernel, (shards, head_size, heads)...]
where the time goes in v3:
time: 101 us
  Pallas kernels  99.5 us (99%)
  local copies, waits for them, and re-layouts  1.32 us (1%)
    pallas_call x1, Pallas kernels, cycle_of_two(): pl.pallas_call(functools.partial(cycle_kernel, (shards, head_size, heads)...  99.5 us

profile of v3, /device:TPU:0, one launch (start us, length us, event | category | flops | bytes accessed | tf_op | source)
XLA Modules:
  0.0 100.8 jit_solution(6785527288300272704)
XLA Ops:
  0.0 99.5 %cycle.1 = bf16[512,2048]{1,0:T(8,128)(2,1)S(1)} custom-call(bf16[256,4096]{1,0:T(8,128)(2,1)} %bitcast.8, s32[1,512]{1,0:T(1,128)} %bitcast.10, s32[1,512]{1,0:T(1,128)} %bitcast.11, bf16[256,16,256]{2,1,0:T(8,128)(2,1)} %bitcast.9, bf16[1,4096]{1,0:T(2,128)(2,1)} %gain.1, bf16[4096,1280]{1,0:T(8,128)(2,1)} %bitcast.6, bf16[1024,4096]{1,0:T(8,128)(2,1)} %bitcast.7), custom_call_target="tpu_custom_call" | custom-call | tf_op jit(solution)/shard_map/cycle/pallas_call | solution.py:1026
  99.5 1.3 %copy.9 = bf16[512,2048]{1,0:T(8,128)(2,1)} copy(bf16[512,2048]{1,0:T(8,128)(2,1)S(1)} %cycle.1) | data formatting | bytes 4194304

commit v4 on v3

--- a/solution.py
+++ b/solution.py
@@ -254,7 +254,7 @@
     other_rows = pl.ds(pl.multiple_of((1 - shard) * rows, rows), rows)
 
     place_blk = lax.axis_index("blk")
-    chips = wd_send.shape[0]
+    chips = up_send.shape[0]
     chip = place_blk // 2
     core = place_blk % 2
     chunk_rows = wx.shape[0] // (2 * chips * CHUNKS)
@@ -340,7 +340,7 @@
         return remote(
             wo_hbm.at[at, pl.ds(first, size)],
             wx.at[at, pl.ds(0, size)],
-            wy_send.at[chunk],
+            wy_send,
             wy_recv.at[chunk],
             {"section": along},
         )
@@ -350,25 +350,32 @@
 
     def weight_in(layer, chunk):
         part = wx.at[chunk_at(place_blk, chunk), held_size(layer)]
-        return remote(part, part, wy_send.at[chunk], wy_recv.at[chunk], {"section": along})
+        return remote(part, part, wy_send, wy_recv.at[chunk], {"section": along})
 
     def upward(layer, owner, chunk):
         part = wx.at[chunk_at(owner * 2 + core, chunk), held_size(layer)]
         return remote(
-            part, part, up_send.at[owner, chunk], up_recv.at[owner, chunk], {"blk": above}
+            part, part, up_send.at[owner], up_recv.at[owner, chunk], {"blk": above}
         )
 
     def downward(layer, owner, chunk):
         part = wx.at[chunk_at(owner * 2 + core, chunk), held_size(layer)]
         return remote(
-            part, part, dn_send.at[owner, chunk], dn_recv.at[owner, chunk], {"blk": below}
-        )
-
-    def sideways(layer, owner, chunk, holder):
-        part = wx.at[chunk_at(owner * 2 + holder, chunk), held_size(layer)]
-        return remote(
-            part, part, wd_send.at[owner, chunk], wd_recv.at[owner, chunk], {"blk": beside}
-        )
+            part, part, dn_send.at[owner], dn_recv.at[owner, chunk], {"blk": below}
+        )
+
+    def sideways(layer, owner, chunk):
+        part = wx.at[chunk_at(owner * 2 + core, chunk), held_size(layer)]
+        return remote(part, part, wd_send, wd_recv, {"blk": beside})
+
+    def all_sideways(layer):
+        part = wx.at[pl.ds(0, wx.shape[0] // 2), held_size(layer)]
+        return remote(part, part, wd_send, wd_recv, {"blk": beside})
+
+    def owned(owner, size):
+        rows_held = CHUNKS * chunk_rows
+        first = pl.multiple_of((owner * 2 + core) * rows_held, rows_held)
+        return wx.at[pl.ds(first, rows_held), pl.ds(0, size)]
 
     def spread(layer, chunk):
         weight_in(layer, chunk).wait_recv()
@@ -381,7 +388,7 @@
         def _():
             downward(layer, chip, chunk).start()
 
-        sideways(layer, chip, chunk, core).start()
+        sideways(layer, chip, chunk).start()
 
     def from_below(layer, distance, chunk):
         owner = chip - distance
@@ -394,7 +401,7 @@
             def _():
                 upward(layer, owner, chunk).start()
 
-            sideways(layer, owner, chunk, core).start()
+            sideways(layer, owner, chunk).start()
 
     def from_above(layer, distance, chunk):
         owner = chip + distance
@@ -407,7 +414,7 @@
             def _():
                 downward(layer, owner, chunk).start()
 
-            sideways(layer, owner, chunk, core).start()
+            sideways(layer, owner, chunk).start()
 
     def pass_on(layer, distance, chunk):
         @pl.when(has_above)
@@ -430,29 +437,36 @@
                 from_above(layer, distance, chunk)
 
     def gathered(layer):
+        all_sideways(layer).wait_recv()
+
+    def settle_weights(layer):
+        held = wide if layer == 1 else span
+        mine = owned(chip, wide if layer == 0 else span)
+        remote(mine, mine, wy_send, wy_recv.at[0], {"section": along}).wait_send()
+        all_sideways(layer).wait_send()
         for owner in range(chips):
-            for chunk in range(CHUNKS):
-                sideways(layer, owner, chunk, 1 - core).wait_recv()
-
-    def settle_weights(layer):
-        for chunk in range(CHUNKS):
-            weight_out(layer, chunk).wait_send()
-            for owner in range(chips):
-                sideways(layer, owner, chunk, core).wait_send()
-
-                @pl.when(has_above & (owner <= chip))
-                def _():
-                    upward(layer, owner, chunk).wait_send()
-
-                @pl.when(has_below & (owner >= chip))
-                def _():
-                    downward(layer, owner, chunk).wait_send()
+            part = owned(owner, held)
+
+            @pl.when(has_above & (owner <= chip))
+            def _():
+                remote(
+                    part, part, up_send.at[owner], up_recv.at[owner, 0], {"blk": above}
+                ).wait_send()
+
+            @pl.when(has_below & (owner >= chip))
+            def _():
+                remote(
+                    part, part, dn_send.at[owner], dn_recv.at[owner, 0], {"blk": below}
+                ).wait_send()
+
+    def sent(part, send, receive):
+        remote(part, part, send, receive.at[0], {"section": along}).wait_send()
 
     def hidden_copy(i):
         return remote(
             hidden.at[pl.ds(i * BLOCK, BLOCK)],
             stage.at[half + i],
-            h_send.at[i],
+            h_send,
             h_recv.at[i],
             {"section": along},
         )
@@ -461,7 +475,7 @@
         return remote(
             ready.at[i, :, pl.ds(0, size)],
             stage.at[i, :, pl.ds(0, size)],
-            lo_send.at[i],
+            lo_send.at[0 if size == span else 1],
             lo_recv.at[i],
             {"section": along},
         )
@@ -471,7 +485,7 @@
         return remote(
             ready.at[i, :, cols],
             stage.at[i, :, cols],
-            hi_send.at[i],
+            hi_send,
             hi_recv.at[i],
             {"section": along},
         )
@@ -480,7 +494,7 @@
         return remote(
             att.at[i, sent_rows],
             att_in.at[i, sent_rows],
-            r_send.at[i],
+            r_send,
             r_recv.at[i],
             {"section": along},
         )
@@ -489,8 +503,8 @@
         return remote(
             att.at[i, sent_rows],
             att_in.at[i, sent_rows],
-            d_send.at[i],
-            d_recv.at[i],
+            d_send,
+            d_recv,
             {"section": corner},
         )
 
@@ -498,7 +512,7 @@
         return remote(
             att_in.at[i, sent_rows],
             att_in.at[i, sent_rows],
-            x_send.at[i],
+            x_send,
             x_recv.at[i],
             {"section": across},
         )
@@ -509,14 +523,14 @@
 
     def partial_copy(i):
         return remote(
-            psend.at[i], precv.at[i], p_send.at[i], p_recv.at[i], {"section": across}
+            psend.at[i], precv.at[i], p_send, p_recv.at[i], {"section": across}
         )
 
     def attended_copy(i, sent_rows):
         return remote(
             att.at[i, sent_rows],
             att.at[i, sent_rows],
-            a_send.at[i],
+            a_send,
             a_recv.at[i],
             {"section": across},
         )
@@ -777,44 +791,25 @@
                 for j in range(count):
                     out[token_rows(i + j), cols] = now[j * BLOCK : (j + 1) * BLOCK]
 
-        def drain(i, carry):
-            partial_copy(i).wait_send()
-            attended_copy(i, own_rows).wait_send()
-
-            @pl.when(i < half)
-            def _():
-                low_copy(i, span).wait_send()
-                high_copy(i).wait_send()
-
-            @pl.when(i >= half)
-            def _():
-                branch_copy(i, own_rows).wait_send()
-                if low:
-                    low_copy(i, low).wait_send()
-
-            return carry
-
-        def unrelay(i, carry):
-            @pl.when(i != half - 1)
-            def _():
-                relay_copy(i, own_rows).wait_send()
-
-            return carry
-
         finish(0, 2)
         settle_weights(0)
-        lax.fori_loop(0, MICRO, drain, 0)
         relay(half)
         relay(half + 1)
         finish(2, 1)
         relay(half + 2)
         finish(half, 2)
         relay(half + 3)
-        lax.fori_loop(0, half + 2, unrelay, 0)
+        sent(psend, p_send, p_recv)
+        sent(att.at[:, own_rows], a_send, a_recv)
+        sent(att.at[pl.ds(half, half), own_rows], r_send, r_recv)
+        early = pl.ds(0, half)
+        sent(ready.at[early, :, pl.ds(0, span)], lo_send.at[0], lo_recv)
+        sent(ready.at[early, :, pl.ds(span, span)], hi_send, hi_recv)
+        if low:
+            sent(ready.at[early, :, pl.ds(0, low)], lo_send.at[1], lo_recv)
         finish(half + 2, 2)
         finish(half - 1, 1)
-
-        lax.fori_loop(half + 2, MICRO, unrelay, 0)
+        sent(att_in.at[pl.ds(0, MICRO - 1), own_rows], x_send, x_recv)
 
     def second_layer():
         hidden_copy(0).start()
@@ -941,14 +936,12 @@
             return carry
 
         lax.fori_loop(0, half // 2, pair, 0)
-        total = first_half(half - 1, 4)
-
         def last(t, carry):
             i = jnp.where(t < half, half + t, half - 1)
 
             @pl.when(t == 2)
             def _():
-                second_half(half - 1, 4, total)
+                second_half(half - 1, 4, first_half(half - 1, 4))
                 for j in range(half, half + 2):
                     attended_copy(j, own_rows).start()
 
@@ -970,32 +963,13 @@
         for j in (half + 2, half + 3, half - 1):
             attended_copy(j, own_rows).start()
         settle_weights(1)
-
-        def drain(i, carry):
-            partial_copy(i).wait_send()
-            branch_copy(i, own_rows).wait_send()
-
-            @pl.when(i < half)
-            def _():
-                hidden_copy(i).wait_send()
-
-            @pl.when(i >= half)
-            def _():
-                relay_copy(i, own_rows).wait_send()
-
-            return carry
-
-        lax.fori_loop(0, MICRO, drain, 0)
-
-        def settle(i, carry):
-            update(i)
-            attended_copy(i, own_rows).wait_send()
-            return carry
-
-        lax.fori_loop(half, MICRO, settle, 0)
-        settle(half - 1, 0)
-        for i in range(half - 1):
-            attended_copy(i, own_rows).wait_send()
+        sent(psend, p_send, p_recv)
+        sent(stage.at[pl.ds(half, half)], h_send, h_recv)
+        sent(att_in.at[pl.ds(half, half), own_rows], x_send, x_recv)
+        lax.fori_loop(half, MICRO, lambda i, carry: update(i), None)
+        update(half - 1)
+        sent(att.at[:, own_rows], r_send, r_recv)
+        sent(att.at[:, own_rows], a_send, a_recv)
         corner_copy(half - 1, own_rows).wait_send()
 
     @pl.when(seg == 0)
@@ -1020,6 +994,8 @@
     tokens = exit_layer.shape[0]
     hbm = pl.BlockSpec(memory_space=pltpu.HBM)
     vmem = pl.BlockSpec(memory_space=pltpu.VMEM)
+    one = pltpu.SemaphoreType.DMA
+    few = pltpu.SemaphoreType.DMA((MICRO // 2,))
     dma = pltpu.SemaphoreType.DMA((MICRO,))
     pieces = pltpu.SemaphoreType.DMA((chips, CHUNKS))
     bf16 = jnp.bfloat16
@@ -1044,12 +1020,32 @@
             pltpu.VMEM((query_width, wide), bf16),
             pltpu.VMEM((MICRO, BLOCK, query_width), bf16),
             pltpu.SemaphoreType.DMA((3,)),
+            few,
+            one,
+            pltpu.SemaphoreType.DMA((CHUNKS,)),
+            pltpu.SemaphoreType.DMA((chips,)),
+            pieces,
+            pltpu.SemaphoreType.DMA((chips,)),
+            pieces,
+            one,
+            one,
+            one,
+            few,
+            pltpu.SemaphoreType.DMA((2,)),
             dma,
-            pltpu.SemaphoreType.DMA((CHUNKS,)),
-            pltpu.SemaphoreType.DMA((CHUNKS,)),
-        ]
-        + [pieces] * 6
-        + [dma] * 16,
+            one,
+            few,
+            one,
+            dma,
+            one,
+            dma,
+            one,
+            dma,
+            one,
+            one,
+            one,
+            dma,
+        ],
         compiler_params=pltpu.CompilerParams(
             collective_id=0, has_side_effects=True, vmem_limit_bytes=VMEM_LIMIT
         ),

time: 101 us -> 98 us (0.970)
  Pallas kernels: 99.5 us -> 96.4 us
    pallas_call x1, Pallas kernels: 99.5 us -> 96.4 us  [cycle_of_two(): pl.pallas_call(functools.partial(cycle_kernel, (shards, head_size, heads)...]
where the time goes in v4:
time: 98 us; the launch traced here: 97.7 us
  Pallas kernels  96.4 us (98%)
  local copies, waits for them, and re-layouts  1.32 us (1%)
    pallas_call x1, Pallas kernels, cycle_of_two(): pl.pallas_call(functools.partial(cycle_kernel, (shards, head_size, heads)...  96.4 us

profile of v4, /device:TPU:0, one launch (start us, length us, event | category | flops | bytes accessed | tf_op | source)
XLA Modules:
  0.0 97.7 jit_solution(7828515229630527508)
XLA Ops:
  0.0 96.4 %cycle.1 = bf16[512,2048]{1,0:T(8,128)(2,1)S(1)} custom-call(bf16[256,4096]{1,0:T(8,128)(2,1)} %bitcast.8, s32[1,512]{1,0:T(1,128)} %bitcast.10, s32[1,512]{1,0:T(1,128)} %bitcast.11, bf16[256,16,256]{2,1,0:T(8,128)(2,1)} %bitcast.9, bf16[1,4096]{1,0:T(2,128)(2,1)} %gain.1, bf16[4096,1280]{1,0:T(8,128)(2,1)} %bitcast.6, bf16[1024,4096]{1,0:T(8,128)(2,1)} %bitcast.7), custom_call_target="tpu_custom_call" | custom-call | tf_op jit(solution)/shard_map/cycle/pallas_call | solution.py:1002
  96.4 1.3 %copy.9 = bf16[512,2048]{1,0:T(8,128)(2,1)} copy(bf16[512,2048]{1,0:T(8,128)(2,1)S(1)} %cycle.1) | data formatting | bytes 4194304

commit v5 on v4

--- a/solution.py
+++ b/solution.py
@@ -180,6 +180,7 @@
 
 MESH = pl.DeviceIdType.MESH
 CHUNKS = 4
+LIGHT = 4
 EARLY = 3
 
 
@@ -233,6 +234,7 @@
     d_recv,
     x_send,
     x_recv,
+    e_send,
 ):
     shards, head_size, heads = sizes
     index = lax.axis_index("section")
@@ -257,7 +259,8 @@
     chips = up_send.shape[0]
     chip = place_blk // 2
     core = place_blk % 2
-    chunk_rows = wx.shape[0] // (2 * chips * CHUNKS)
+    units = CHUNKS + LIGHT
+    chunk_rows = wx.shape[0] // (chips * units)
     above = jnp.minimum(chip + 1, chips - 1) * 2 + core
     below = jnp.maximum(chip - 1, 0) * 2 + core
     beside = chip * 2 + 1 - core
@@ -331,11 +334,21 @@
         return table[token_rows(i), :][:, 0:1]
 
     def chunk_at(owner, chunk):
-        first = pl.multiple_of(owner * (CHUNKS * chunk_rows) + chunk * chunk_rows, chunk_rows)
-        return pl.ds(first, chunk_rows)
+        first = (owner * units + core * LIGHT + chunk) * chunk_rows
+        return pl.ds(pl.multiple_of(first, chunk_rows), chunk_rows)
+
+    def carried(chunk, action):
+        if chunk < LIGHT:
+            action()
+        else:
+            pl.when(core == 1)(action)
+
+    def by_core(action):
+        pl.when(core == 0)(functools.partial(action, LIGHT))
+        pl.when(core == 1)(functools.partial(action, CHUNKS))
 
     def weight_out(layer, chunk):
-        at = chunk_at(place_blk, chunk)
+        at = chunk_at(chip, chunk)
         first, size = (low, wide) if layer == 0 else (0, span)
         return remote(
             wo_hbm.at[at, pl.ds(first, size)],
@@ -349,35 +362,38 @@
         return pl.ds(0, wide if layer == 1 else span)
 
     def weight_in(layer, chunk):
-        part = wx.at[chunk_at(place_blk, chunk), held_size(layer)]
+        part = wx.at[chunk_at(chip, chunk), held_size(layer)]
         return remote(part, part, wy_send, wy_recv.at[chunk], {"section": along})
 
     def upward(layer, owner, chunk):
-        part = wx.at[chunk_at(owner * 2 + core, chunk), held_size(layer)]
+        part = wx.at[chunk_at(owner, chunk), held_size(layer)]
         return remote(
             part, part, up_send.at[owner], up_recv.at[owner, chunk], {"blk": above}
         )
 
     def downward(layer, owner, chunk):
-        part = wx.at[chunk_at(owner * 2 + core, chunk), held_size(layer)]
+        part = wx.at[chunk_at(owner, chunk), held_size(layer)]
         return remote(
             part, part, dn_send.at[owner], dn_recv.at[owner, chunk], {"blk": below}
         )
 
     def sideways(layer, owner, chunk):
-        part = wx.at[chunk_at(owner * 2 + core, chunk), held_size(layer)]
+        part = wx.at[chunk_at(owner, chunk), held_size(layer)]
         return remote(part, part, wd_send, wd_recv, {"blk": beside})
 
-    def all_sideways(layer):
-        part = wx.at[pl.ds(0, wx.shape[0] // 2), held_size(layer)]
+    def all_sideways(layer, count):
+        part = wx.at[pl.ds(0, chips * count * chunk_rows), held_size(layer)]
         return remote(part, part, wd_send, wd_recv, {"blk": beside})
 
-    def owned(owner, size):
-        rows_held = CHUNKS * chunk_rows
-        first = pl.multiple_of((owner * 2 + core) * rows_held, rows_held)
-        return wx.at[pl.ds(first, rows_held), pl.ds(0, size)]
-
-    def spread(layer, chunk):
+    def owned(owner, count, size):
+        first = (owner * units + core * LIGHT) * chunk_rows
+        rows_held = pl.ds(pl.multiple_of(first, chunk_rows), count * chunk_rows)
+        return wx.at[rows_held, pl.ds(0, size)]
+
+    def send_weights(layer, chunk):
+        carried(chunk, lambda: weight_out(layer, chunk).start())
+
+    def spread_held(layer, chunk):
         weight_in(layer, chunk).wait_recv()
 
         @pl.when(has_above)
@@ -416,7 +432,7 @@
 
             sideways(layer, owner, chunk).start()
 
-    def pass_on(layer, distance, chunk):
+    def pass_held(layer, distance, chunk):
         @pl.when(has_above)
         def _():
             from_below(layer, distance, chunk)
@@ -425,27 +441,39 @@
         def _():
             from_above(layer, distance, chunk)
 
+    def collect_held(layer, chunk):
+        for distance in range(1, chips):
+
+            @pl.when(jnp.logical_not(has_above))
+            def _():
+                from_below(layer, distance, chunk)
+
+            @pl.when(jnp.logical_not(has_below))
+            def _():
+                from_above(layer, distance, chunk)
+
+    def spread(layer, chunk):
+        carried(chunk, functools.partial(spread_held, layer, chunk))
+
+    def pass_on(layer, distance, chunk):
+        carried(chunk, functools.partial(pass_held, layer, distance, chunk))
+
     def collect(layer, chunk):
-        for distance in range(1, chips):
-
-            @pl.when(jnp.logical_not(has_above))
-            def _():
-                from_below(layer, distance, chunk)
-
-            @pl.when(jnp.logical_not(has_below))
-            def _():
-                from_above(layer, distance, chunk)
+        carried(chunk, functools.partial(collect_held, layer, chunk))
 
     def gathered(layer):
-        all_sideways(layer).wait_recv()
+        by_core(lambda count: all_sideways(layer, units - count).wait_recv())
 
     def settle_weights(layer):
+        by_core(functools.partial(settle_held, layer))
+
+    def settle_held(layer, count):
         held = wide if layer == 1 else span
-        mine = owned(chip, wide if layer == 0 else span)
+        mine = owned(chip, count, wide if layer == 0 else span)
         remote(mine, mine, wy_send, wy_recv.at[0], {"section": along}).wait_send()
-        all_sideways(layer).wait_send()
+        all_sideways(layer, count).wait_send()
         for owner in range(chips):
-            part = owned(owner, held)
+            part = owned(owner, count, held)
 
             @pl.when(has_above & (owner <= chip))
             def _():
@@ -487,6 +515,25 @@
             stage.at[i, :, cols],
             hi_send,
             hi_recv.at[i],
+            {"section": along},
+        )
+
+    def high_part(part):
+        cols = pl.ds(span + part * (span // 2), span // 2)
+        return remote(
+            ready.at[half - 1, :, cols],
+            stage.at[half - 1, :, cols],
+            hi_send,
+            hi_recv.at[half - 1 + part],
+            {"section": along},
+        )
+
+    def echo_copy(i):
+        return remote(
+            att_in.at[i, other_rows],
+            att.at[i, other_rows],
+            e_send,
+            a_recv.at[i],
             {"section": along},
         )
 
@@ -652,7 +699,7 @@
 
     def first_layer():
         for chunk in range(CHUNKS):
-            weight_out(0, chunk).start()
+            send_weights(0, chunk)
         for i in range(1, half):
             own_copy(i).start()
         load_wo.start()
@@ -684,7 +731,8 @@
             @pl.when(i == MICRO - 1)
             def _():
                 low_copy(half - 1, span).start()
-                high_copy(half - 1).start()
+                for part in range(2):
+                    high_part(part).start()
 
         def step(t, carry):
             i = turn(0, t)
@@ -779,7 +827,7 @@
                 if j == half - 1:
                     branch_copy(j, own_rows).wait_recv()
                     corner_copy(j, other_rows).wait_recv()
-                else:
+                elif j not in (half, half + 1):
                     relay_copy(j, other_rows).wait_recv()
             source = att_in[pl.ds(i, count)].reshape(count * BLOCK, query_width)
             deep = jnp.concatenate([depths(j) for j in range(i, i + count)], axis=0) > 1
@@ -796,6 +844,9 @@
         relay(half)
         relay(half + 1)
         finish(2, 1)
+        for j in (half, half + 1):
+            relay_copy(j, other_rows).wait_recv()
+            echo_copy(j).start()
         relay(half + 2)
         finish(half, 2)
         relay(half + 3)
@@ -810,15 +861,16 @@
         finish(half + 2, 2)
         finish(half - 1, 1)
         sent(att_in.at[pl.ds(0, MICRO - 1), own_rows], x_send, x_recv)
+        sent(att_in.at[pl.ds(half, 2), other_rows], e_send, a_recv)
 
     def second_layer():
         hidden_copy(0).start()
         for chunk in range(EARLY):
-            weight_out(1, chunk).start()
+            send_weights(1, chunk)
         for i in range(1, half):
             hidden_copy(i).start()
         for chunk in range(EARLY, CHUNKS):
-            weight_out(1, chunk).start()
+            send_weights(1, chunk)
         for i in range(half):
             rest_copy(i).start()
         load_wo.start()
@@ -829,13 +881,12 @@
 
         def first_half(i, slot):
             low_copy(i, span).wait_recv()
-            total = scale(i, 1, 0, span)
+            keep_squares(slot, 1, scale(i, 1, 0, span))
             multiply(slot, 1, 0, span, False)
-            return total
-
-        def second_half(i, slot, total):
+
+        def second_half(i, slot):
             high_copy(i).wait_recv()
-            total = total + scale(i, 1, span, width)
+            total = squares[slot][:, :1] + scale(i, 1, span, width)
             multiply(slot, 1, span, width, True)
             keep_squares(slot, 1, total)
             send_partial(i, slot)
@@ -902,7 +953,7 @@
                 for j in range(2):
                     relay(half + j)
 
-            total = first_half(t, t % 2)
+            first_half(t, t % 2)
 
             @pl.when(t == half - 2)
             def _():
@@ -910,7 +961,7 @@
                 for chunk in range(CHUNKS):
                     collect(1, chunk)
 
-            second_half(t, t % 2, total)
+            second_half(t, t % 2)
 
             @pl.when(t > 0)
             def _():
@@ -936,14 +987,20 @@
             return carry
 
         lax.fori_loop(0, half // 2, pair, 0)
+        def next_part(part):
+            high_part(part).wait_recv()
+            first = span + part * (span // 2)
+            total = squares[4][:, :1] + scale(half - 1, 1, first, first + span // 2)
+            multiply(4, 1, first, first + span // 2, True)
+            keep_squares(4, 1, total)
+
         def last(t, carry):
             i = jnp.where(t < half, half + t, half - 1)
 
             @pl.when(t == 2)
             def _():
-                second_half(half - 1, 4, first_half(half - 1, 4))
-                for j in range(half, half + 2):
-                    attended_copy(j, own_rows).start()
+                first_half(half - 1, 4)
+                next_part(0)
 
             attend_rows(i, jnp.where(t < half, (t + 2) % 4, 4))
 
@@ -953,6 +1010,12 @@
 
             branch_copy(i, own_rows).start()
 
+            @pl.when(t == 2)
+            def _():
+                next_part(1)
+                send_partial(half - 1, 4)
+                attended_copy(i, own_rows).start()
+
             @pl.when(t == half - 1)
             def _():
                 update(half - 2)
@@ -960,7 +1023,7 @@
             return carry
 
         lax.fori_loop(0, half + 1, last, 0)
-        for j in (half + 2, half + 3, half - 1):
+        for j in (half + 3, half - 1):
             attended_copy(j, own_rows).start()
         settle_weights(1)
         sent(psend, p_send, p_recv)
@@ -969,7 +1032,7 @@
         lax.fori_loop(half, MICRO, lambda i, carry: update(i), None)
         update(half - 1)
         sent(att.at[:, own_rows], r_send, r_recv)
-        sent(att.at[:, own_rows], a_send, a_recv)
+        sent(att.at[pl.ds(0, MICRO - 2), own_rows], a_send, a_recv)
         corner_copy(half - 1, own_rows).wait_send()
 
     @pl.when(seg == 0)
@@ -1034,7 +1097,7 @@
             pltpu.SemaphoreType.DMA((2,)),
             dma,
             one,
-            few,
+            pltpu.SemaphoreType.DMA((MICRO // 2 + 1,)),
             one,
             dma,
             one,
@@ -1045,6 +1108,7 @@
             one,
             one,
             dma,
+            one,
         ],
         compiler_params=pltpu.CompilerParams(
             collective_id=0, has_side_effects=True, vmem_limit_bytes=VMEM_LIMIT

time: 98 us -> 97 us (0.990)
  Pallas kernels: 96.4 us -> 95.4 us
    pallas_call x1, Pallas kernels: 96.4 us -> 95.4 us  [cycle_of_two(): pl.pallas_call(functools.partial(cycle_kernel, (shards, head_size, heads)...]
where the time goes in v5:
time: 97 us; the launch traced here: 96.7 us
  Pallas kernels  95.4 us (98%)
  local copies, waits for them, and re-layouts  1.32 us (1%)
    pallas_call x1, Pallas kernels, cycle_of_two(): pl.pallas_call(functools.partial(cycle_kernel, (shards, head_size, heads)...  95.4 us

profile of v5, /device:TPU:0, one launch (start us, length us, event | category | flops | bytes accessed | tf_op | source)
XLA Modules:
  0.0 96.7 jit_solution(16382066434434763019)
XLA Ops:
  0.0 95.4 %cycle.1 = bf16[512,2048]{1,0:T(8,128)(2,1)S(1)} custom-call(bf16[256,4096]{1,0:T(8,128)(2,1)} %bitcast.8, s32[1,512]{1,0:T(1,128)} %bitcast.10, s32[1,512]{1,0:T(1,128)} %bitcast.11, bf16[256,16,256]{2,1,0:T(8,128)(2,1)} %bitcast.9, bf16[1,4096]{1,0:T(2,128)(2,1)} %gain.1, bf16[4096,1280]{1,0:T(8,128)(2,1)} %bitcast.6, bf16[1024,4096]{1,0:T(8,128)(2,1)} %bitcast.7), custom_call_target="tpu_custom_call" | custom-call | tf_op jit(solution)/shard_map/cycle/pallas_call | solution.py:1065
  95.4 1.3 %copy.9 = bf16[512,2048]{1,0:T(8,128)(2,1)} copy(bf16[512,2048]{1,0:T(8,128)(2,1)S(1)} %cycle.1) | data formatting | bytes 4194304

commit v6 on v5

--- a/solution.py
+++ b/solution.py
@@ -528,6 +528,16 @@
             {"section": along},
         )
 
+    def low_part(part):
+        cols = pl.ds(part * (span // 2), span // 2)
+        return remote(
+            ready.at[half - 1, :, cols],
+            stage.at[half - 1, :, cols],
+            lo_send.at[0],
+            lo_recv.at[half - 1 if part else MICRO],
+            {"section": along},
+        )
+
     def echo_copy(i):
         return remote(
             att_in.at[i, other_rows],
@@ -550,8 +560,8 @@
         return remote(
             att.at[i, sent_rows],
             att_in.at[i, sent_rows],
-            d_send,
-            d_recv,
+            d_send.at[0 if i == half - 1 else 1],
+            d_recv.at[0 if i == half - 1 else 1],
             {"section": corner},
         )
 
@@ -730,7 +740,7 @@
 
             @pl.when(i == MICRO - 1)
             def _():
-                low_copy(half - 1, span).start()
+                low_part(1).start()
                 for part in range(2):
                     high_part(part).start()
 
@@ -785,6 +795,10 @@
             @pl.when(i >= half)
             def _():
                 branch_copy(i, own_rows).start()
+
+            @pl.when(i == MICRO - 1)
+            def _():
+                low_part(0).start()
 
             @pl.when(i == half + 1)
             def _():
@@ -824,7 +838,7 @@
 
         def finish(i, count):
             for j in range(i, i + count):
-                if j == half - 1:
+                if j in (half - 1, MICRO - 1):
                     branch_copy(j, own_rows).wait_recv()
                     corner_copy(j, other_rows).wait_recv()
                 elif j not in (half, half + 1):
@@ -849,7 +863,6 @@
             echo_copy(j).start()
         relay(half + 2)
         finish(half, 2)
-        relay(half + 3)
         sent(psend, p_send, p_recv)
         sent(att.at[:, own_rows], a_send, a_recv)
         sent(att.at[pl.ds(half, half), own_rows], r_send, r_recv)
@@ -860,7 +873,7 @@
             sent(ready.at[early, :, pl.ds(0, low)], lo_send.at[1], lo_recv)
         finish(half + 2, 2)
         finish(half - 1, 1)
-        sent(att_in.at[pl.ds(0, MICRO - 1), own_rows], x_send, x_recv)
+        sent(att_in.at[pl.ds(0, MICRO - 2), own_rows], x_send, x_recv)
         sent(att_in.at[pl.ds(half, 2), other_rows], e_send, a_recv)
 
     def second_layer():
@@ -880,7 +893,11 @@
             spread(1, chunk)
 
         def first_half(i, slot):
-            low_copy(i, span).wait_recv()
+            if isinstance(i, int):
+                for part in range(2):
+                    low_part(part).wait_recv()
+            else:
+                low_copy(i, span).wait_recv()
             keep_squares(slot, 1, scale(i, 1, 0, span))
             multiply(slot, 1, 0, span, False)
 
@@ -1000,20 +1017,22 @@
             @pl.when(t == 2)
             def _():
                 first_half(half - 1, 4)
-                next_part(0)
+                for part in range(2):
+                    next_part(part)
+                send_partial(half - 1, 4)
 
             attend_rows(i, jnp.where(t < half, (t + 2) % 4, 4))
 
-            @pl.when(t == half)
-            def _():
-                corner_copy(i, own_rows).start()
+            for j, when in ((MICRO - 1, half - 1), (half - 1, half)):
+
+                @pl.when(t == when)
+                def _():
+                    corner_copy(j, own_rows).start()
 
             branch_copy(i, own_rows).start()
 
             @pl.when(t == 2)
             def _():
-                next_part(1)
-                send_partial(half - 1, 4)
                 attended_copy(i, own_rows).start()
 
             @pl.when(t == half - 1)
@@ -1033,7 +1052,8 @@
         update(half - 1)
         sent(att.at[:, own_rows], r_send, r_recv)
         sent(att.at[pl.ds(0, MICRO - 2), own_rows], a_send, a_recv)
-        corner_copy(half - 1, own_rows).wait_send()
+        for i in (MICRO - 1, half - 1):
+            corner_copy(i, own_rows).wait_send()
 
     @pl.when(seg == 0)
     def _():
@@ -1095,7 +1115,7 @@
             one,
             few,
             pltpu.SemaphoreType.DMA((2,)),
-            dma,
+            pltpu.SemaphoreType.DMA((MICRO + 1,)),
             one,
             pltpu.SemaphoreType.DMA((MICRO // 2 + 1,)),
             one,
@@ -1104,8 +1124,8 @@
             dma,
             one,
             dma,
-            one,
-            one,
+            pltpu.SemaphoreType.DMA((2,)),
+            pltpu.SemaphoreType.DMA((2,)),
             one,
             dma,
             one,

time: 97 us -> 96.5 us (level)
  no operation moved by 1% of the time
where the time goes in v6:
time: 96.5 us; the launch traced here: 96.2 us
  Pallas kernels  94.9 us (98%)
  local copies, waits for them, and re-layouts  1.32 us (1%)
    pallas_call x1, Pallas kernels, cycle_of_two(): pl.pallas_call(functools.partial(cycle_kernel, (shards, head_size, heads)...  94.9 us

profile of v6, /device:TPU:0, one launch (start us, length us, event | category | flops | bytes accessed | tf_op | source)
XLA Modules:
  0.0 96.2 jit_solution(1673623496372628134)
XLA Ops:
  0.0 94.9 %cycle.1 = bf16[512,2048]{1,0:T(8,128)(2,1)S(1)} custom-call(bf16[256,4096]{1,0:T(8,128)(2,1)} %bitcast.8, s32[1,512]{1,0:T(1,128)} %bitcast.10, s32[1,512]{1,0:T(1,128)} %bitcast.11, bf16[256,16,256]{2,1,0:T(8,128)(2,1)} %bitcast.9, bf16[1,4096]{1,0:T(2,128)(2,1)} %gain.1, bf16[4096,1280]{1,0:T(8,128)(2,1)} %bitcast.6, bf16[1024,4096]{1,0:T(8,128)(2,1)} %bitcast.7), custom_call_target="tpu_custom_call" | custom-call | tf_op jit(solution)/shard_map/cycle/pallas_call | solution.py:1085
  94.9 1.3 %copy.9 = bf16[512,2048]{1,0:T(8,128)(2,1)} copy(bf16[512,2048]{1,0:T(8,128)(2,1)S(1)} %cycle.1) | data formatting | bytes 4194304
